TPU v7x, 8 devices: a whole 2x2x1 slice. The times are simulated.
8 devices in a mesh: part: 1 (over z), row: 2 (over y), col: 4 (over x, core).
Axes of the slice: x: 2, y: 2, z: 1, core: 2. Of those that a mesh axis runs over, the one named last changes fastest.
Arguments:
- counts: bfloat16 [8192, 16384], P(('part', 'row'), 'col')
- w_init: float32 [8192, 256], P(('part', 'row'))
- h_init: float32 [256, 16384], P(None, ('part', 'col'))
Outputs:
- output 1: float32 [8192, 256], P(('part', 'row'))
- output 2: float32 [256, 16384], P(None, ('part', 'col'))
All inputs are finite; a program needn't handle non-finite values.
Results may differ from a plain program's by a relative error of at most 0.001.
Values are sent between devices in bfloat16 or wider.
A program may use at most 1 GiB of HBM per device.

v0:
```python
import jax
import jax.numpy as jnp
from jax import lax
from jax.sharding import PartitionSpec as P

SWEEPS = 4
EPS = 1e-6
CONTRACT_WORDS = (((1,), (1,)), ((), ()))
CONTRACT_DOCS = (((0,), (0,)), ((), ()))


def ratio_block(c_blk, w_bf, h_bf):
    z_blk = jnp.dot(w_bf, h_bf, preferred_element_type=jnp.float32)
    return (c_blk.astype(jnp.float32) / (z_blk + EPS)).astype(jnp.bfloat16)


def local_sweeps(c_blk, w_loc, h_loc):
    for sweep_index in range(SWEEPS):
        h_bf = h_loc.astype(jnp.bfloat16)
        q_blk = ratio_block(c_blk, w_loc.astype(jnp.bfloat16), h_bf)
        a_w = lax.psum(lax.dot_general(q_blk, h_bf, CONTRACT_WORDS, preferred_element_type=jnp.float32), 'col')
        s_h = lax.psum(jnp.sum(h_loc, axis=1), 'col')
        w_loc = w_loc * a_w / s_h
        w_bf = w_loc.astype(jnp.bfloat16)
        q_blk = ratio_block(c_blk, w_bf, h_bf)
        a_h = lax.psum(lax.dot_general(w_bf, q_blk, CONTRACT_DOCS, preferred_element_type=jnp.float32), 'row')
        s_w = lax.psum(jnp.sum(w_loc, axis=0), 'row')
        h_loc = h_loc * a_h / s_w[:, None]
    return w_loc, h_loc


def solution(mesh):
    spec_c = P(('part', 'row'), 'col')
    spec_w = P(('part', 'row'), None)
    spec_h = P(None, ('part', 'col'))
    return jax.shard_map(local_sweeps, mesh=mesh, in_specs=(spec_c, spec_w, spec_h), out_specs=(spec_w, spec_h), check_vma=False)
```

profile of v0, /device:TPU:0, one launch (start us, length us, event | category | flops | bytes accessed | tf_op | source)
XLA Modules:
  0.0 1027.3 jit_solution(3131852951094817851)
XLA Ops:
  7.2 28.4 %fusion.22 = f32[4096,256]{1,0:T(8,128)} fusion(bf16[4096,4096]{1,0:T(8,128)(2,1)} %param.3, f32[4096,256]{1,0:T(8,128)} %param.4, f32[256,4096]{1,0:T(8,128)} %param.5), kind=kOutput, calls=%fused_computation.23 | convolution fusion | flops 17250123776 | bytes 46137344 | tf_op jit(solution)/shard_map/dot_general | solution.py:21
  38.2 9.0 psum.113
  47.2 71.3 %all-reduce.9.cloned.1.call-done = f32[4096,256]{1,0:T(8,128)} async-done(((f32[4096,256]{1,0:T(8,128)}), f32[4096,256]{1,0:T(8,128)}) %all-reduce.9.cloned.1.call-update) | async-done | bytes 4194320 | tf_op jit(solution)/shard_map/psum | solution.py:21
  118.5 6.0 fusion.86
  124.6 29.5 %fusion.20 = f32[256,4096]{1,0:T(8,128)} fusion(bf16[4096,4096]{1,0:T(8,128)(2,1)} %param.3, f32[4096,256]{1,0:T(8,128)} %get-tuple-element.15, f32[256,4096]{1,0:T(8,128)} %param.5), kind=kOutput, calls=%fused_computation.22 | convolution fusion | flops 17250123776 | bytes 46137344 | tf_op jit(solution)/shard_map/dot_general | solution.py:26
  154.2 5.1 psum.115
  159.3 97.2 %all-reduce.11.cloned.1.call-done = f32[256,4096]{1,0:T(8,128)} async-done(((f32[256,4096]{1,0:T(8,128)}), f32[256,4096]{1,0:T(8,128)}) %all-reduce.11.cloned.1.call-update) | async-done | bytes 4194320 | tf_op jit(solution)/shard_map/psum | solution.py:26
  256.6 6.0 fusion.85
  262.5 28.4 %fusion.18 = f32[4096,256]{1,0:T(8,128)} fusion(bf16[4096,4096]{1,0:T(8,128)(2,1)} %param.3, f32[256,4096]{1,0:T(8,128)} %get-tuple-element.13, f32[4096,256]{1,0:T(8,128)} %get-tuple-element.15), kind=kOutput, calls=%fused_computation.21 | convolution fusion | flops 17250123776 | bytes 46137344 | tf_op jit(solution)/shard_map/dot_general | solution.py:21
  291.0 6.9 psum.117
  297.9 73.0 %all-reduce.13.cloned.1.call-done = f32[4096,256]{1,0:T(8,128)} async-done(((f32[4096,256]{1,0:T(8,128)}), f32[4096,256]{1,0:T(8,128)}) %all-reduce.13.cloned.1.call-update) | async-done | bytes 4194320 | tf_op jit(solution)/shard_map/psum | solution.py:21
  370.9 6.0 fusion.84
  376.9 29.6 %fusion.16 = f32[256,4096]{1,0:T(8,128)} fusion(bf16[4096,4096]{1,0:T(8,128)(2,1)} %param.3, f32[4096,256]{1,0:T(8,128)} %get-tuple-element.11, f32[256,4096]{1,0:T(8,128)} %get-tuple-element.13), kind=kOutput, calls=%fused_computation.20 | convolution fusion | flops 17250123776 | bytes 46137344 | tf_op jit(solution)/shard_map/dot_general | solution.py:26
  406.6 5.2 psum.119
  411.8 97.2 %all-reduce.15.cloned.1.call-done = f32[256,4096]{1,0:T(8,128)} async-done(((f32[256,4096]{1,0:T(8,128)}), f32[256,4096]{1,0:T(8,128)}) %all-reduce.15.cloned.1.call-update) | async-done | bytes 4194320 | tf_op jit(solution)/shard_map/psum | solution.py:26
  509.0 6.0 fusion.83
  514.9 28.4 %fusion.14 = f32[4096,256]{1,0:T(8,128)} fusion(bf16[4096,4096]{1,0:T(8,128)(2,1)} %param.3, f32[256,4096]{1,0:T(8,128)} %get-tuple-element.9, f32[4096,256]{1,0:T(8,128)} %get-tuple-element.11), kind=kOutput, calls=%fused_computation.19 | convolution fusion | flops 17250123776 | bytes 46137344 | tf_op jit(solution)/shard_map/dot_general | solution.py:21
  543.4 6.9 psum.121
  550.3 73.0 %all-reduce.17.cloned.1.call-done = f32[4096,256]{1,0:T(8,128)} async-done(((f32[4096,256]{1,0:T(8,128)}), f32[4096,256]{1,0:T(8,128)}) %all-reduce.17.cloned.1.call-update) | async-done | bytes 4194320 | tf_op jit(solution)/shard_map/psum | solution.py:21
  623.3 6.0 fusion.82
  629.3 29.6 %fusion.12 = f32[256,4096]{1,0:T(8,128)} fusion(bf16[4096,4096]{1,0:T(8,128)(2,1)} %param.3, f32[4096,256]{1,0:T(8,128)} %get-tuple-element.7, f32[256,4096]{1,0:T(8,128)} %get-tuple-element.9), kind=kOutput, calls=%fused_computation.18 | convolution fusion | flops 17250123776 | bytes 46137344 | tf_op jit(solution)/shard_map/dot_general | solution.py:26
  659.0 5.2 psum.123
  664.2 97.1 %all-reduce.19.cloned.1.call-done = f32[256,4096]{1,0:T(8,128)} async-done(((f32[256,4096]{1,0:T(8,128)}), f32[256,4096]{1,0:T(8,128)}) %all-reduce.19.cloned.1.call-update) | async-done | bytes 4194320 | tf_op jit(solution)/shard_map/psum | solution.py:26
  761.4 5.9 fusion.81
  767.3 28.3 %fusion.10 = f32[4096,256]{1,0:T(8,128)} fusion(bf16[4096,4096]{1,0:T(8,128)(2,1)} %param.3, f32[256,4096]{1,0:T(8,128)} %get-tuple-element.5, f32[4096,256]{1,0:T(8,128)} %get-tuple-element.7), kind=kOutput, calls=%fused_computation.17 | convolution fusion | flops 17250123776 | bytes 46137344 | tf_op jit(solution)/shard_map/dot_general | solution.py:21
  795.6 6.9 psum.125
  802.5 73.0 %all-reduce.21.cloned.1.call-done = f32[4096,256]{1,0:T(8,128)} async-done(((f32[4096,256]{1,0:T(8,128)}), f32[4096,256]{1,0:T(8,128)}) %all-reduce.21.cloned.1.call-update) | async-done | bytes 4194320 | tf_op jit(solution)/shard_map/psum | solution.py:21
  875.5 6.0 fusion.80
  881.5 29.5 %fusion.8 = f32[256,4096]{1,0:T(8,128)} fusion(bf16[4096,4096]{1,0:T(8,128)(2,1)} %param.3, f32[4096,256]{1,0:T(8,128)} %get-tuple-element.3, f32[256,4096]{1,0:T(8,128)} %get-tuple-element.5), kind=kOutput, calls=%fused_computation.16 | convolution fusion | flops 17250123776 | bytes 46137344 | tf_op jit(solution)/shard_map/dot_general | solution.py:26
  911.1 5.0 psum.127
  916.0 97.4 %all-reduce.23.cloned.1.call-done = f32[256,4096]{1,0:T(8,128)} async-done(((f32[256,4096]{1,0:T(8,128)}), f32[256,4096]{1,0:T(8,128)}) %all-reduce.23.cloned.1.call-update) | async-done | bytes 4194320 | tf_op jit(solution)/shard_map/psum | solution.py:26
  1013.5 6.5 multiply_divide_fusion
  (17 shorter events, 2.9 us)
Async XLA Ops:
  7.2 111.4 %all-reduce.9.cloned.1.call-start = ((), (), s32[]{:S(2)}) async-start(), calls=%async_computation | async-start | bytes 8388608 | tf_op jit(solution)/shard_map/psum | solution.py:21
  35.7 220.9 %all-reduce.11.cloned.1.call-start = ((), (), s32[]{:S(2)}) async-start(), calls=%async_computation.1 | async-start | bytes 8388608 | tf_op jit(solution)/shard_map/psum | solution.py:26
  154.1 216.7 %all-reduce.13.cloned.1.call-start = ((), (), s32[]{:S(2)}) async-start(), calls=%async_computation.2 | async-start | bytes 8388608 | tf_op jit(solution)/shard_map/psum | solution.py:21
  290.9 218.0 %all-reduce.15.cloned.1.call-start = ((), (), s32[]{:S(2)}) async-start(), calls=%async_computation.3 | async-start | bytes 8388608 | tf_op jit(solution)/shard_map/psum | solution.py:26
  406.5 216.7 %all-reduce.17.cloned.1.call-start = ((), (), s32[]{:S(2)}) async-start(), calls=%async_computation.4 | async-start | bytes 8388608 | tf_op jit(solution)/shard_map/psum | solution.py:21
  543.3 218.0 %all-reduce.19.cloned.1.call-start = ((), (), s32[]{:S(2)}) async-start(), calls=%async_computation.5 | async-start | bytes 8388608 | tf_op jit(solution)/shard_map/psum | solution.py:26
  658.9 216.6 %all-reduce.21.cloned.1.call-start = ((), (), s32[]{:S(2)}) async-start(), calls=%async_computation.6 | async-start | bytes 8388608 | tf_op jit(solution)/shard_map/psum | solution.py:21
  795.6 217.9 %all-reduce.23.cloned.1.call-start = ((), (), s32[]{:S(2)}) async-start(), calls=%async_computation.7 | async-start | bytes 8388608 | tf_op jit(solution)/shard_map/psum | solution.py:26
Sparse Core Ops, SparseCore 0:
  35.8 82.6 all-reduce.8
  154.2 102.2 all-reduce.10
  291.0 79.7 all-reduce.12
  406.7 102.2 all-reduce.14
  543.5 79.7 all-reduce.16
  659.1 102.2 all-reduce.18
  795.7 79.7 all-reduce.20
  911.2 102.2 all-reduce.22
where the time goes:
time: 1040 us; the launch traced here: 1030 us
  waiting for transfers between devices  679 us (65%)
  matrix products  232 us (22%)
  other arithmetic  51 us (5%)
  blocking collectives  50.2 us (5%)
  between operations  14.6 us (1%)
    psum x4, waiting for transfers between devices, local_sweeps(): lax.psum(lax.dot_general(w_bf, q_blk, CONTRACT_DOCS, preferred_element_ty...  389 us
    psum x4, waiting for transfers between devices, local_sweeps(): lax.psum(lax.dot_general(q_blk, h_bf, CONTRACT_WORDS, preferred_element_t...  290 us
    dot_general x4, matrix products, local_sweeps(): lax.dot_general(w_bf, q_blk, CONTRACT_DOCS, preferred_element_type=jnp.fl...  118 us
    dot_general x4, matrix products, local_sweeps(): lax.dot_general(q_blk, h_bf, CONTRACT_WORDS, preferred_element_type=jnp.f...  113 us
    psum x4, blocking collectives, local_sweeps(): s_h = lax.psum(jnp.sum(h_loc, axis=1), 'col')  29.7 us
    reduce_sum x4, other arithmetic, local_sweeps(): s_w = lax.psum(jnp.sum(w_loc, axis=0), 'row')  24.1 us
  transfers between devices with their start and end apart: 8, of which 8 were waited for; matrix products, arithmetic and copies ran while one was open for 0% of the time, Pallas kernels for 0%

commit v1 on v0

v1 whole, which is shorter than its diff:
```python
import functools

import jax
import jax.numpy as jnp
from jax import lax
from jax.experimental import pallas as pl
from jax.experimental.pallas import tpu as pltpu
from jax.sharding import PartitionSpec as P

SWEEPS = 4
EPS = 1e-6
ND = 8
NV = 8
LANES = 128
MESH = pl.DeviceIdType.MESH
F32 = jnp.float32
BF16 = jnp.bfloat16


def kernel(
    rows, cols, c_hbm, w_hbm, h_hbm, w_out, h_out,
    c_v, w_bf, w_t, h_bf, h_t, w_f, h_f, a_w, a_h, r_a, r_x, r_y,
    sw_acc, sw_slots, sw_col, sh_acc, sh_part, sh_slots, sh_row,
    load_sem, c_sem,
    a_send, a_recv, x_send, x_recv, g_send, g_recv, p_send, p_recv, q_send, q_recv,
    y_send, y_recv, z_send, z_recv, sw_send, sw_recv, sh_send, sh_recv,
    wo_send, wo_recv, ho_send, ho_recv, ow_sem, oh_sem,
):
    docs, words = c_v.shape
    topics = w_bf.shape[1]
    dt, vt, kh = docs // ND, words // NV, topics // 2
    half, quarter = dt // 2, dt // 4
    n_dev = rows * cols
    y, i = lax.axis_index("row"), lax.axis_index("col")
    x, core = i // 2, i % 2
    me = y * cols + i
    partner = {"col": x * 2 + (1 - core)}
    across = {"col": (1 - x) * 2 + core}
    above = {"row": 1 - y}

    def peer(step):
        other = (me + step) % n_dev
        return {"row": other // cols, "col": other % cols}

    def rows_at(start, size):
        return pl.ds(pl.multiple_of(start, size), size)

    def remote(src, dst, send, recv, device):
        return pltpu.make_async_remote_copy(
            src_ref=src, dst_ref=dst, send_sem=send, recv_sem=recv, device_id=device, device_id_type=MESH)

    def mine(d):
        return rows_at(d * dt + core * half + x * quarter, quarter)

    def theirs(d):
        return rows_at(d * dt + core * half + (1 - x) * quarter, quarter)

    def copy_a(d):
        return remote(a_w.at[rows_at(d * dt + (1 - core) * half, half)], r_a.at[rows_at(d * half, half)],
                      a_send.at[d], a_recv.at[d], partner)

    def copy_x(d):
        return remote(a_w.at[theirs(d)], r_x.at[rows_at(d * quarter, quarter)], x_send.at[d], x_recv.at[d], across)

    def copy_g(d):
        return remote(w_bf.at[mine(d)], w_bf.at[mine(d)], g_send.at[d], g_recv.at[d], across)

    def copy_p(d):
        return remote(w_bf.at[mine(d)], w_bf.at[mine(d)], p_send.at[d], p_recv.at[d], partner)

    def copy_q(d):
        return remote(w_bf.at[theirs(d)], w_bf.at[theirs(d)], q_send.at[d], q_recv.at[d], partner)

    own_k, other_k = rows_at(y * kh, kh), rows_at((1 - y) * kh, kh)

    def words_at(v):
        return rows_at(v * vt, vt)

    def copy_y(v):
        return remote(a_h.at[other_k, words_at(v)], r_y.at[:, words_at(v)], y_send.at[v], y_recv.at[v], above)

    def copy_z(v):
        return remote(h_bf.at[own_k, words_at(v)], h_bf.at[own_k, words_at(v)], z_send.at[v], z_recv.at[v], above)

    def copy_sw(step):
        return remote(sw_acc, sw_slots.at[me], sw_send.at[step - 1], sw_recv.at[step - 1], peer(step))

    def copy_sh(step):
        return remote(sh_part, sh_slots.at[me], sh_send.at[step - 1], sh_recv.at[step - 1], peer(step))

    def copy_wo(d, step):
        k = d * (cols - 1) + step - 1
        return remote(w_f.at[rows_at(d * quarter, quarter)], w_out.at[mine(d)], wo_send.at[k], wo_recv.at[k],
                      {"col": (i + step) % cols})

    def copy_ho(v):
        return remote(h_f.at[:, words_at(v)], h_out.at[own_k, words_at(v)], ho_send.at[v], ho_recv.at[v], above)

    def out_w(d):
        return pltpu.make_async_copy(w_f.at[rows_at(d * quarter, quarter)], w_out.at[mine(d)], ow_sem.at[d])

    def out_h(v):
        return pltpu.make_async_copy(h_f.at[:, words_at(v)], h_out.at[own_k, words_at(v)], oh_sem.at[v])

    def load_c(d):
        return pltpu.make_async_copy(c_hbm.at[rows_at(d * dt, dt)], c_v.at[rows_at(d * dt, dt)], c_sem.at[d])

    def each(count, body):
        def step(n, carry):
            body(n)
            return carry
        lax.fori_loop(0, count, step, 0)

    def ratio(d, v):
        z = jnp.dot(w_bf[rows_at(d * dt, dt), :], h_bf[:, words_at(v)], preferred_element_type=F32)
        return (c_v[rows_at(d * dt, dt), words_at(v)].astype(F32) / (z + EPS)).astype(BF16)

    def w_tile(d, v):
        part = jnp.dot(ratio(d, v), h_t[words_at(v), :], preferred_element_type=F32)
        held = a_w[rows_at(d * dt, dt), :]
        a_w[rows_at(d * dt, dt), :] = jnp.where(v == 0, 0.0, held) + part

    def h_tile(d, v):
        part = jnp.dot(w_t[...], ratio(d, v), preferred_element_type=F32)
        held = a_h[:, words_at(v)]
        a_h[:, words_at(v)] = jnp.where(d == 0, 0.0, held) + part

    def fold_lanes(block):
        total = block[:, :LANES]
        for g in range(1, block.shape[1] // LANES):
            total = total + block[:, g * LANES:(g + 1) * LANES]
        return total

    def send_sh():
        sh_part[...] = jnp.sum(sh_acc[...].T.reshape(LANES // 8, 8, kh), axis=0)
        sh_slots[me] = sh_part[...]
        for step in range(1, n_dev):
            copy_sh(step).start()

    def take_sh():
        for step in range(1, n_dev):
            copy_sh(step).wait()
        for r in range(rows):
            total = sh_slots[r * cols]
            for n in range(1, cols):
                total = total + sh_slots[r * cols + n]
            sh_row[:, r * kh:(r + 1) * kh] = jnp.broadcast_to(jnp.sum(total, axis=0, keepdims=True), (8, kh))

    def send_sw():
        sw_slots[me] = sw_acc[...]
        for step in range(1, n_dev):
            copy_sw(step).start()

    def take_sw():
        for step in range(1, n_dev):
            copy_sw(step).wait()
        total = sw_slots[0]
        for n in range(1, n_dev):
            total = total + sw_slots[n]
        total = jnp.sum(total, axis=0, keepdims=True)
        own = jnp.where(y == 0, total[:, :kh], total[:, kh:])
        sw_col[...] = jnp.broadcast_to(own, (LANES, kh)).T

    load_h = pltpu.make_async_copy(h_hbm, a_h, load_sem.at[0])
    load_w = pltpu.make_async_copy(w_hbm, a_w, load_sem.at[1])
    load_h.start()
    load_w.start()
    for d in range(ND):
        load_c(d).start()
    barrier = pltpu.get_barrier_semaphore()
    for step in range(1, n_dev):
        pl.semaphore_signal(barrier, inc=1, device_id=peer(step), device_id_type=MESH)
    pl.semaphore_wait(barrier, n_dev - 1)

    load_h.wait()
    sh_acc[...] = jnp.zeros_like(sh_acc)

    def start_h(v):
        h_bf[:, words_at(v)] = a_h[:, words_at(v)].astype(BF16)
        own = a_h[own_k, words_at(v)]
        h_f[:, words_at(v)] = own
        sh_acc[...] += fold_lanes(own)
        h_t[words_at(v), :] = h_bf[:, words_at(v)].T

    each(NV, start_h)
    send_sh()
    load_w.wait()

    def start_w(d):
        w_bf[rows_at(d * dt, dt), :] = a_w[rows_at(d * dt, dt), :].astype(BF16)
        w_f[rows_at(d * quarter, quarter), :] = a_w[mine(d), :]

    each(ND, start_w)

    def sweep_body(sweep, carry):
        last = sweep == SWEEPS - 1

        def s0(d):
            @pl.when(sweep == 0)
            def _():
                load_c(d).wait()

            def tile(v, carry):
                w_tile(d, v)
                return carry
            lax.fori_loop(jnp.where(sweep == 0, 0, NV - 1), NV, tile, 0)
            copy_a(d).start()

        def s1(d):
            copy_a(d).wait_recv()
            own = rows_at(d * dt + core * half, half)
            a_w[own, :] += r_a[rows_at(d * half, half), :]
            copy_x(d).start()

        def s2(d):
            @pl.when(d == 0)
            def _():
                take_sh()
                sw_acc[...] = jnp.zeros_like(sw_acc)
            copy_x(d).wait_recv()
            own = rows_at(d * quarter, quarter)
            fresh = w_f[own, :] * (a_w[mine(d), :] + r_x[own, :]) / sh_row[0:1, :]
            w_f[own, :] = fresh
            w_bf[mine(d), :] = fresh.astype(BF16)
            copy_g(d).start()
            copy_p(d).start()
            sw_acc[...] += jnp.sum(fresh.reshape(quarter // 8, 8, topics), axis=0)

            @pl.when(d == ND - 1)
            def _():
                send_sw()

        def s3(d):
            copy_g(d).wait_recv()
            copy_q(d).start()

        def s5(d):
            copy_p(d).wait_recv()
            copy_q(d).wait_recv()
            w_t[...] = w_bf[rows_at(d * dt, dt), :].T

            def tile(v):
                h_tile(d, v)

                @pl.when(jnp.logical_and(d == ND - 1, v < 2))
                def _():
                    copy_y(v).start()
            each(NV, tile)

        def stage(it, lag, body):
            @pl.when(jnp.logical_and(it >= lag, it < lag + ND))
            def _():
                body(it - lag)

        def w_step(it):
            stage(it, 0, s0)
            stage(it, 1, s1)
            stage(it, 3, s2)
            stage(it, 5, s5)
            stage(it, 4, s3)

        each(ND + 5, w_step)

        def w_sent(d):
            copy_a(d).wait_send()
            copy_x(d).wait_send()
            copy_g(d).wait_send()
            copy_p(d).wait_send()
            copy_q(d).wait_send()

        each(ND, w_sent)

        @pl.when(last)
        def _():
            def give(d):
                out_w(d).start()
                for step in range(1, cols):
                    copy_wo(d, step).start()
            each(ND, give)

        def t1(v):
            @pl.when(v == 0)
            def _():
                take_sw()
                sh_acc[...] = jnp.zeros_like(sh_acc)
            copy_y(v).wait_recv()
            for g in range(vt // LANES):
                at = pl.ds(pl.multiple_of(v * vt + g * LANES, LANES), LANES)
                fresh = h_f[:, at] * (a_h[own_k, at] + r_y[:, at]) / sw_col[...]
                h_f[:, at] = fresh
                h_bf[own_k, at] = fresh.astype(BF16)
                sh_acc[...] += fresh

            @pl.when(jnp.logical_not(last))
            def _():
                copy_z(v).start()

                @pl.when(v == NV - 1)
                def _():
                    send_sh()

            @pl.when(last)
            def _():
                out_h(v).start()
                copy_ho(v).start()

            @pl.when(v + 2 < NV)
            def _():
                copy_y(v + 2).start()

        def t3(v):
            copy_z(v).wait_recv()
            h_t[words_at(v), :] = h_bf[:, words_at(v)].T

            @pl.when(v < NV - 1)
            def _():
                each(ND, lambda d: w_tile(d, v))

        def h_step(it):
            @pl.when(it < NV)
            def _():
                t1(it)

            @pl.when(jnp.logical_and(it >= 1, jnp.logical_not(last)))
            def _():
                t3(it - 1)

        each(NV + 1, h_step)

        def h_sent(v):
            copy_y(v).wait_send()

            @pl.when(jnp.logical_not(last))
            def _():
                copy_z(v).wait_send()

        each(NV, h_sent)
        return carry

    lax.fori_loop(0, SWEEPS, sweep_body, 0)

    def finish_w(d):
        out_w(d).wait()
        for step in range(1, cols):
            copy_wo(d, step).wait()

    def finish_h(v):
        out_h(v).wait()
        copy_ho(v).wait()

    each(ND, finish_w)
    each(NV, finish_h)


def solution(mesh):
    rows, cols = mesh.shape["row"], mesh.shape["col"]
    n_dev = rows * cols

    def local(c_blk, w_loc, h_loc):
        docs, words = c_blk.shape
        topics = w_loc.shape[1]
        vmem = pltpu.VMEM
        dma = pltpu.SemaphoreType.DMA
        scratch = [
            vmem((docs, words), BF16),
            vmem((docs, topics), BF16),
            vmem((topics, docs // ND), BF16),
            vmem((topics, words), BF16),
            vmem((words, topics), BF16),
            vmem((docs // 4, topics), F32),
            vmem((topics // 2, words), F32),
            vmem((docs, topics), F32),
            vmem((topics, words), F32),
            vmem((docs // 2, topics), F32),
            vmem((docs // 4, topics), F32),
            vmem((topics // 2, words), F32),
            vmem((8, topics), F32),
            vmem((n_dev, 8, topics), F32),
            vmem((topics // 2, LANES), F32),
            vmem((topics // 2, LANES), F32),
            vmem((8, topics // 2), F32),
            vmem((n_dev, 8, topics // 2), F32),
            vmem((8, topics), F32),
            dma((2,)),
            dma((ND,)),
        ]
        scratch += [dma((ND,))] * 10
        scratch += [dma((NV,))] * 4
        scratch += [dma((n_dev - 1,))] * 4
        scratch += [dma((ND * (cols - 1),))] * 2
        scratch += [dma((NV,))] * 2
        scratch += [dma((ND,)), dma((NV,))]
        any_space = pl.BlockSpec(memory_space=pl.ANY)
        return pl.pallas_call(
            functools.partial(kernel, rows, cols),
            out_shape=(jax.ShapeDtypeStruct(w_loc.shape, F32), jax.ShapeDtypeStruct(h_loc.shape, F32)),
            in_specs=[any_space] * 3,
            out_specs=(any_space, any_space),
            scratch_shapes=scratch,
            compiler_params=pltpu.CompilerParams(
                collective_id=0, has_side_effects=True, vmem_limit_bytes=67_043_328),
            name="nmf",
        )(c_blk, w_loc, h_loc)

    spec_c = P(("part", "row"), "col")
    spec_w = P(("part", "row"), None)
    spec_h = P(None, ("part", "col"))
    return jax.shard_map(local, mesh=mesh, in_specs=(spec_c, spec_w, spec_h), out_specs=(spec_w, spec_h), check_vma=False)
```

time: 1040 us -> 562 us (0.54); the launches traced: 1030 us -> 562 us
  waiting for transfers between devices: 679 us -> 0 us
  Pallas kernels: 0 us -> 555 us
  matrix products: 232 us -> 0 us
  other arithmetic: 51 us -> 0 us
  blocking collectives: 50.2 us -> 0 us
  between operations: 14.6 us -> 0.65 us
    psum x8 -> x0, waiting for transfers between devices: 679 us -> none  [the longest x4 389 us: local_sweeps(): lax.psum(lax.dot_general(w_bf, q_blk, CONTRACT_DOCS, preferred_element_ty...]
    pallas_call x0 -> x1, Pallas kernels: none -> 555 us  [local(): pl.pallas_call(functools.partial(kernel, rows, cols), out_shape=(jax.Shap...]
    dot_general x8 -> x0, matrix products: 232 us -> none  [the longest x4 118 us: local_sweeps(): lax.dot_general(w_bf, q_blk, CONTRACT_DOCS, preferred_element_type=jnp.fl...]
    psum x8 -> x0, blocking collectives: 50.2 us -> none  [the longest x4 29.7 us: local_sweeps(): s_h = lax.psum(jnp.sum(h_loc, axis=1), 'col')]
    reduce_sum x8 -> x0, other arithmetic: 44.5 us -> none  [the longest x4 24.1 us: local_sweeps(): s_w = lax.psum(jnp.sum(w_loc, axis=0), 'row')]
  transfers between devices with their start and end apart: 8 -> 0, of which waited for: 8 -> 0; matrix products, arithmetic and copies ran while one was open for 0% -> 0% of each run, Pallas kernels for 0% -> 0%
where the time goes in v1:
time: 562 us
  Pallas kernels  555 us (99%)
  local copies, waits for them, and re-layouts  6.66 us (1%)
    pallas_call x1, Pallas kernels, local(): pl.pallas_call(functools.partial(kernel, rows, cols), out_shape=(jax.Shap...  555 us

profile of v1, /device:TPU:0, one launch (start us, length us, event | category | flops | bytes accessed | tf_op | source)
XLA Modules:
  0.0 562.4 jit_solution(7760803791909735356)
XLA Ops:
  0.6 555.1 %nmf.1 = (f32[4096,256]{1,0:T(8,128)}, f32[256,4096]{1,0:T(8,128)}) custom-call(bf16[4096,4096]{1,0:T(8,128)(2,1)} %c_hbm.1, f32[4096,256]{1,0:T(8,128)} %w_hbm.1, f32[256,4096]{1,0:T(8,128)} %h_hbm.1), custom_call_target="tpu_custom_call" | custom-call | tf_op jit(solution)/shard_map/nmf/pallas_call | solution.py:394
  555.7 0.0 copy-start
  555.7 4.6 copy.7
  560.3 0.0 copy-done
  560.3 2.0 copy.8
Async XLA Ops:
  555.7 4.7 copy-start

commit v2 on v1

--- a/solution.py
+++ b/solution.py
@@ -21,7 +21,7 @@
     rows, cols, c_hbm, w_hbm, h_hbm, w_out, h_out,
     c_v, w_bf, w_t, h_bf, h_t, w_f, h_f, a_w, a_h, r_a, r_x, r_y,
     sw_acc, sw_slots, sw_col, sh_acc, sh_part, sh_slots, sh_row,
-    load_sem, c_sem,
+    load_sem, h_sem, c_sem,
     a_send, a_recv, x_send, x_recv, g_send, g_recv, p_send, p_recv, q_send, q_recv,
     y_send, y_recv, z_send, z_recv, sw_send, sw_recv, sh_send, sh_recv,
     wo_send, wo_recv, ho_send, ho_recv, ow_sem, oh_sem,
@@ -77,10 +77,10 @@
         return rows_at(v * vt, vt)
 
     def copy_y(v):
-        return remote(a_h.at[other_k, words_at(v)], r_y.at[:, words_at(v)], y_send.at[v], y_recv.at[v], above)
+        return remote(a_h.at[v, other_k], r_y.at[v], y_send.at[v], y_recv.at[v], above)
 
     def copy_z(v):
-        return remote(h_bf.at[own_k, words_at(v)], h_bf.at[own_k, words_at(v)], z_send.at[v], z_recv.at[v], above)
+        return remote(h_bf.at[v, own_k], h_bf.at[v, own_k], z_send.at[v], z_recv.at[v], above)
 
     def copy_sw(step):
         return remote(sw_acc, sw_slots.at[me], sw_send.at[step - 1], sw_recv.at[step - 1], peer(step))
@@ -94,13 +94,13 @@
                       {"col": (i + step) % cols})
 
     def copy_ho(v):
-        return remote(h_f.at[:, words_at(v)], h_out.at[own_k, words_at(v)], ho_send.at[v], ho_recv.at[v], above)
+        return remote(h_f.at[v], h_out.at[own_k, words_at(v)], ho_send.at[v], ho_recv.at[v], above)
 
     def out_w(d):
         return pltpu.make_async_copy(w_f.at[rows_at(d * quarter, quarter)], w_out.at[mine(d)], ow_sem.at[d])
 
     def out_h(v):
-        return pltpu.make_async_copy(h_f.at[:, words_at(v)], h_out.at[own_k, words_at(v)], oh_sem.at[v])
+        return pltpu.make_async_copy(h_f.at[v], h_out.at[own_k, words_at(v)], oh_sem.at[v])
 
     def load_c(d):
         return pltpu.make_async_copy(c_hbm.at[rows_at(d * dt, dt)], c_v.at[rows_at(d * dt, dt)], c_sem.at[d])
@@ -112,7 +112,7 @@
         lax.fori_loop(0, count, step, 0)
 
     def ratio(d, v):
-        z = jnp.dot(w_bf[rows_at(d * dt, dt), :], h_bf[:, words_at(v)], preferred_element_type=F32)
+        z = jnp.dot(w_bf[rows_at(d * dt, dt), :], h_bf[v], preferred_element_type=F32)
         return (c_v[rows_at(d * dt, dt), words_at(v)].astype(F32) / (z + EPS)).astype(BF16)
 
     def w_tile(d, v):
@@ -122,8 +122,8 @@
 
     def h_tile(d, v):
         part = jnp.dot(w_t[...], ratio(d, v), preferred_element_type=F32)
-        held = a_h[:, words_at(v)]
-        a_h[:, words_at(v)] = jnp.where(d == 0, 0.0, held) + part
+        held = a_h[v]
+        a_h[v] = jnp.where(d == 0, 0.0, held) + part
 
     def fold_lanes(block):
         total = block[:, :LANES]
@@ -161,9 +161,11 @@
         own = jnp.where(y == 0, total[:, :kh], total[:, kh:])
         sw_col[...] = jnp.broadcast_to(own, (LANES, kh)).T
 
-    load_h = pltpu.make_async_copy(h_hbm, a_h, load_sem.at[0])
-    load_w = pltpu.make_async_copy(w_hbm, a_w, load_sem.at[1])
-    load_h.start()
+    def load_h(v):
+        return pltpu.make_async_copy(h_hbm.at[:, words_at(v)], a_h.at[v], h_sem.at[v])
+
+    load_w = pltpu.make_async_copy(w_hbm, a_w, load_sem.at[0])
+    each(NV, lambda v: load_h(v).start())
     load_w.start()
     for d in range(ND):
         load_c(d).start()
@@ -172,15 +174,15 @@
         pl.semaphore_signal(barrier, inc=1, device_id=peer(step), device_id_type=MESH)
     pl.semaphore_wait(barrier, n_dev - 1)
 
-    load_h.wait()
     sh_acc[...] = jnp.zeros_like(sh_acc)
 
     def start_h(v):
-        h_bf[:, words_at(v)] = a_h[:, words_at(v)].astype(BF16)
-        own = a_h[own_k, words_at(v)]
-        h_f[:, words_at(v)] = own
+        load_h(v).wait()
+        h_bf[v] = a_h[v].astype(BF16)
+        own = a_h[v, own_k]
+        h_f[v] = own
         sh_acc[...] += fold_lanes(own)
-        h_t[words_at(v), :] = h_bf[:, words_at(v)].T
+        h_t[words_at(v), :] = h_bf[v].T
 
     each(NV, start_h)
     send_sh()
@@ -285,10 +287,10 @@
                 sh_acc[...] = jnp.zeros_like(sh_acc)
             copy_y(v).wait_recv()
             for g in range(vt // LANES):
-                at = pl.ds(pl.multiple_of(v * vt + g * LANES, LANES), LANES)
-                fresh = h_f[:, at] * (a_h[own_k, at] + r_y[:, at]) / sw_col[...]
-                h_f[:, at] = fresh
-                h_bf[own_k, at] = fresh.astype(BF16)
+                at = slice(g * LANES, (g + 1) * LANES)
+                fresh = h_f[v, :, at] * (a_h[v, own_k, at] + r_y[v, :, at]) / sw_col[...]
+                h_f[v, :, at] = fresh
+                h_bf[v, own_k, at] = fresh.astype(BF16)
                 sh_acc[...] += fresh
 
             @pl.when(jnp.logical_not(last))
@@ -310,7 +312,7 @@
 
         def t3(v):
             copy_z(v).wait_recv()
-            h_t[words_at(v), :] = h_bf[:, words_at(v)].T
+            h_t[words_at(v), :] = h_bf[v].T
 
             @pl.when(v < NV - 1)
             def _():
@@ -365,15 +367,15 @@
             vmem((docs, words), BF16),
             vmem((docs, topics), BF16),
             vmem((topics, docs // ND), BF16),
-            vmem((topics, words), BF16),
+            vmem((NV, topics, words // NV), BF16),
             vmem((words, topics), BF16),
             vmem((docs // 4, topics), F32),
-            vmem((topics // 2, words), F32),
+            vmem((NV, topics // 2, words // NV), F32),
             vmem((docs, topics), F32),
-            vmem((topics, words), F32),
+            vmem((NV, topics, words // NV), F32),
             vmem((docs // 2, topics), F32),
             vmem((docs // 4, topics), F32),
-            vmem((topics // 2, words), F32),
+            vmem((NV, topics // 2, words // NV), F32),
             vmem((8, topics), F32),
             vmem((n_dev, 8, topics), F32),
             vmem((topics // 2, LANES), F32),
@@ -381,7 +383,8 @@
             vmem((8, topics // 2), F32),
             vmem((n_dev, 8, topics // 2), F32),
             vmem((8, topics), F32),
-            dma((2,)),
+            dma((1,)),
+            dma((NV,)),
             dma((ND,)),
         ]
         scratch += [dma((ND,))] * 10

time: 562 us -> 559 us (level)
  no operation moved by 1% of the time
where the time goes in v2:
time: 559 us
  Pallas kernels  552 us (99%)
  local copies, waits for them, and re-layouts  6.66 us (1%)
    pallas_call x1, Pallas kernels, local(): pl.pallas_call(functools.partial(kernel, rows, cols), out_shape=(jax.Shap...  552 us

profile of v2, /device:TPU:0, one launch (start us, length us, event | category | flops | bytes accessed | tf_op | source)
XLA Modules:
  0.0 559.0 jit_solution(11768567664726681433)
XLA Ops:
  0.6 551.7 %nmf.1 = (f32[4096,256]{1,0:T(8,128)}, f32[256,4096]{1,0:T(8,128)}) custom-call(bf16[4096,4096]{1,0:T(8,128)(2,1)} %c_hbm.1, f32[4096,256]{1,0:T(8,128)} %w_hbm.1, f32[256,4096]{1,0:T(8,128)} %h_hbm.1), custom_call_target="tpu_custom_call" | custom-call | tf_op jit(solution)/shard_map/nmf/pallas_call | solution.py:397
  552.3 0.0 copy-start
  552.3 4.6 copy.7
  557.0 0.0 copy-done
  557.0 2.0 copy.8
Async XLA Ops:
  552.3 4.7 copy-start

commit v3 on v2

--- a/solution.py
+++ b/solution.py
@@ -11,6 +11,7 @@
 EPS = 1e-6
 ND = 8
 NV = 8
+GROUP = 4
 LANES = 128
 MESH = pl.DeviceIdType.MESH
 F32 = jnp.float32
@@ -202,10 +203,16 @@
             def _():
                 load_c(d).wait()
 
-            def tile(v, carry):
-                w_tile(d, v)
-                return carry
-            lax.fori_loop(jnp.where(sweep == 0, 0, NV - 1), NV, tile, 0)
+            @pl.when(sweep == 0)
+            def _():
+                def group(n):
+                    for k in range(GROUP):
+                        w_tile(d, n * GROUP + k)
+                each(NV // GROUP, group)
+
+            @pl.when(sweep > 0)
+            def _():
+                w_tile(d, NV - 1)
             copy_a(d).start()
 
         def s1(d):
@@ -241,13 +248,15 @@
             copy_q(d).wait_recv()
             w_t[...] = w_bf[rows_at(d * dt, dt), :].T
 
-            def tile(v):
-                h_tile(d, v)
-
-                @pl.when(jnp.logical_and(d == ND - 1, v < 2))
+            def group(n):
+                for k in range(GROUP):
+                    h_tile(d, n * GROUP + k)
+
+                @pl.when(jnp.logical_and(d == ND - 1, n == 0))
                 def _():
-                    copy_y(v).start()
-            each(NV, tile)
+                    copy_y(0).start()
+                    copy_y(1).start()
+            each(NV // GROUP, group)
 
         def stage(it, lag, body):
             @pl.when(jnp.logical_and(it >= lag, it < lag + ND))
@@ -316,7 +325,10 @@
 
             @pl.when(v < NV - 1)
             def _():
-                each(ND, lambda d: w_tile(d, v))
+                def group(n):
+                    for k in range(GROUP):
+                        w_tile(n * GROUP + k, v)
+                each(ND // GROUP, group)
 
         def h_step(it):
             @pl.when(it < NV)

time: 559 us -> 524 us (0.937)
  Pallas kernels: 552 us -> 516 us
    pallas_call x1, Pallas kernels: 552 us -> 516 us  [local(): pl.pallas_call(functools.partial(kernel, rows, cols), out_shape=(jax.Shap...]
where the time goes in v3:
time: 524 us
  Pallas kernels  516 us (98%)
  local copies, waits for them, and re-layouts  6.66 us (1%)
    pallas_call x1, Pallas kernels, local(): pl.pallas_call(functools.partial(kernel, rows, cols), out_shape=(jax.Shap...  516 us

profile of v3, /device:TPU:0, one launch (start us, length us, event | category | flops | bytes accessed | tf_op | source)
XLA Modules:
  0.0 523.5 jit_solution(16808705958599341074)
XLA Ops:
  0.6 516.2 %nmf.1 = (f32[4096,256]{1,0:T(8,128)}, f32[256,4096]{1,0:T(8,128)}) custom-call(bf16[4096,4096]{1,0:T(8,128)(2,1)} %c_hbm.1, f32[4096,256]{1,0:T(8,128)} %w_hbm.1, f32[256,4096]{1,0:T(8,128)} %h_hbm.1), custom_call_target="tpu_custom_call" | custom-call | tf_op jit(solution)/shard_map/nmf/pallas_call | solution.py:409
  516.9 0.0 copy-start
  516.9 4.6 copy.7
  521.5 0.0 copy-done
  521.5 2.0 copy.8
Async XLA Ops:
  516.9 4.7 copy-start

commit v4 on v3

--- a/solution.py
+++ b/solution.py
@@ -12,6 +12,7 @@
 ND = 8
 NV = 8
 GROUP = 4
+LAG1, LAG2, LAG3, LAG5 = 2, 4, 5, 6
 LANES = 128
 MESH = pl.DeviceIdType.MESH
 F32 = jnp.float32
@@ -264,13 +265,10 @@
                 body(it - lag)
 
         def w_step(it):
-            stage(it, 0, s0)
-            stage(it, 1, s1)
-            stage(it, 3, s2)
-            stage(it, 5, s5)
-            stage(it, 4, s3)
-
-        each(ND + 5, w_step)
+            for lag, body in ((LAG2, s2), (LAG1, s1), (0, s0), (LAG3, s3), (LAG5, s5)):
+                stage(it, lag, body)
+
+        each(ND + LAG5, w_step)
 
         def w_sent(d):
             copy_a(d).wait_send()

time: 524 us -> 510 us (0.973)
  Pallas kernels: 516 us -> 502 us
    pallas_call x1, Pallas kernels: 516 us -> 502 us  [local(): pl.pallas_call(functools.partial(kernel, rows, cols), out_shape=(jax.Shap...]
where the time goes in v4:
time: 510 us
  Pallas kernels  502 us (98%)
  local copies, waits for them, and re-layouts  6.66 us (1%)
    pallas_call x1, Pallas kernels, local(): pl.pallas_call(functools.partial(kernel, rows, cols), out_shape=(jax.Shap...  502 us

profile of v4, /device:TPU:0, one launch (start us, length us, event | category | flops | bytes accessed | tf_op | source)
XLA Modules:
  0.0 509.7 jit_solution(17244823388253161881)
XLA Ops:
  0.6 502.4 %nmf.1 = (f32[4096,256]{1,0:T(8,128)}, f32[256,4096]{1,0:T(8,128)}) custom-call(bf16[4096,4096]{1,0:T(8,128)(2,1)} %c_hbm.1, f32[4096,256]{1,0:T(8,128)} %w_hbm.1, f32[256,4096]{1,0:T(8,128)} %h_hbm.1), custom_call_target="tpu_custom_call" | custom-call | tf_op jit(solution)/shard_map/nmf/pallas_call | solution.py:407
  503.0 0.0 copy-start
  503.0 4.6 copy.7
  507.6 0.0 copy-done
  507.6 2.0 copy.8
Async XLA Ops:
  503.0 4.7 copy-start

commit v5 on v4

--- a/solution.py
+++ b/solution.py
@@ -23,7 +23,7 @@
     rows, cols, c_hbm, w_hbm, h_hbm, w_out, h_out,
     c_v, w_bf, w_t, h_bf, h_t, w_f, h_f, a_w, a_h, r_a, r_x, r_y,
     sw_acc, sw_slots, sw_col, sh_acc, sh_part, sh_slots, sh_row,
-    load_sem, h_sem, c_sem,
+    w_sem, h_sem, c_sem,
     a_send, a_recv, x_send, x_recv, g_send, g_recv, p_send, p_recv, q_send, q_recv,
     y_send, y_recv, z_send, z_recv, sw_send, sw_recv, sh_send, sh_recv,
     wo_send, wo_recv, ho_send, ho_recv, ow_sem, oh_sem,
@@ -117,15 +117,20 @@
         z = jnp.dot(w_bf[rows_at(d * dt, dt), :], h_bf[v], preferred_element_type=F32)
         return (c_v[rows_at(d * dt, dt), words_at(v)].astype(F32) / (z + EPS)).astype(BF16)
 
+    def select(first, held):
+        if isinstance(first, bool):
+            return jnp.zeros_like(held) if first else held
+        return jnp.where(first, 0.0, held)
+
     def w_tile(d, v):
         part = jnp.dot(ratio(d, v), h_t[words_at(v), :], preferred_element_type=F32)
         held = a_w[rows_at(d * dt, dt), :]
-        a_w[rows_at(d * dt, dt), :] = jnp.where(v == 0, 0.0, held) + part
+        a_w[rows_at(d * dt, dt), :] = select(v == 0, held) + part
 
     def h_tile(d, v):
         part = jnp.dot(w_t[...], ratio(d, v), preferred_element_type=F32)
         held = a_h[v]
-        a_h[v] = jnp.where(d == 0, 0.0, held) + part
+        a_h[v] = select(d == 0, held) + part
 
     def fold_lanes(block):
         total = block[:, :LANES]
@@ -166,16 +171,15 @@
     def load_h(v):
         return pltpu.make_async_copy(h_hbm.at[:, words_at(v)], a_h.at[v], h_sem.at[v])
 
-    load_w = pltpu.make_async_copy(w_hbm, a_w, load_sem.at[0])
-    each(NV, lambda v: load_h(v).start())
-    load_w.start()
-    for d in range(ND):
-        load_c(d).start()
+    def load_w(d):
+        return pltpu.make_async_copy(w_hbm.at[rows_at(d * dt, dt)], a_w.at[rows_at(d * dt, dt)], w_sem.at[d])
+
     barrier = pltpu.get_barrier_semaphore()
     for step in range(1, n_dev):
         pl.semaphore_signal(barrier, inc=1, device_id=peer(step), device_id_type=MESH)
-    pl.semaphore_wait(barrier, n_dev - 1)
-
+    each(NV, lambda v: load_h(v).start())
+    load_w(0).start()
+    load_c(0).start()
     sh_acc[...] = jnp.zeros_like(sh_acc)
 
     def start_h(v):
@@ -186,15 +190,20 @@
         sh_acc[...] += fold_lanes(own)
         h_t[words_at(v), :] = h_bf[v].T
 
+        @pl.when(v + 1 < ND)
+        def _():
+            load_w(v + 1).start()
+            load_c(v + 1).start()
+
     each(NV, start_h)
+    pl.semaphore_wait(barrier, n_dev - 1)
     send_sh()
-    load_w.wait()
 
     def start_w(d):
+        load_w(d).wait()
         w_bf[rows_at(d * dt, dt), :] = a_w[rows_at(d * dt, dt), :].astype(BF16)
         w_f[rows_at(d * quarter, quarter), :] = a_w[mine(d), :]
-
-    each(ND, start_w)
+        load_c(d).wait()
 
     def sweep_body(sweep, carry):
         last = sweep == SWEEPS - 1
@@ -202,14 +211,9 @@
         def s0(d):
             @pl.when(sweep == 0)
             def _():
-                load_c(d).wait()
-
-            @pl.when(sweep == 0)
-            def _():
-                def group(n):
-                    for k in range(GROUP):
-                        w_tile(d, n * GROUP + k)
-                each(NV // GROUP, group)
+                start_w(d)
+                for v in range(NV):
+                    w_tile(d, v)
 
             @pl.when(sweep > 0)
             def _():
@@ -249,15 +253,22 @@
             copy_q(d).wait_recv()
             w_t[...] = w_bf[rows_at(d * dt, dt), :].T
 
-            def group(n):
-                for k in range(GROUP):
-                    h_tile(d, n * GROUP + k)
-
-                @pl.when(jnp.logical_and(d == ND - 1, n == 0))
-                def _():
-                    copy_y(0).start()
-                    copy_y(1).start()
-            each(NV // GROUP, group)
+            @pl.when(d < ND - 1)
+            def _():
+                for v in range(NV):
+                    h_tile(d, v)
+
+            @pl.when(d == ND - 1)
+            def _():
+                def group(n):
+                    h_tile(d, 2 * n)
+                    h_tile(d, 2 * n + 1)
+
+                    @pl.when(n == 0)
+                    def _():
+                        copy_y(0).start()
+                        copy_y(1).start()
+                each(NV // 2, group)
 
         def stage(it, lag, body):
             @pl.when(jnp.logical_and(it >= lag, it < lag + ND))
@@ -393,7 +404,7 @@
             vmem((8, topics // 2), F32),
             vmem((n_dev, 8, topics // 2), F32),
             vmem((8, topics), F32),
-            dma((1,)),
+            dma((ND,)),
             dma((NV,)),
             dma((ND,)),
         ]

time: 510 us -> 496 us (0.973)
  Pallas kernels: 502 us -> 488 us
    pallas_call x1, Pallas kernels: 502 us -> 488 us  [local(): pl.pallas_call(functools.partial(kernel, rows, cols), out_shape=(jax.Shap...]
where the time goes in v5:
time: 496 us; the launch traced here: 495 us
  Pallas kernels  488 us (98%)
  local copies, waits for them, and re-layouts  6.66 us (1%)
    pallas_call x1, Pallas kernels, local(): pl.pallas_call(functools.partial(kernel, rows, cols), out_shape=(jax.Shap...  488 us

profile of v5, /device:TPU:0, one launch (start us, length us, event | category | flops | bytes accessed | tf_op | source)
XLA Modules:
  0.0 495.4 jit_solution(9573045945721633740)
XLA Ops:
  0.6 488.1 %nmf.1 = (f32[4096,256]{1,0:T(8,128)}, f32[256,4096]{1,0:T(8,128)}) custom-call(bf16[4096,4096]{1,0:T(8,128)(2,1)} %c_hbm.1, f32[4096,256]{1,0:T(8,128)} %w_hbm.1, f32[256,4096]{1,0:T(8,128)} %h_hbm.1), custom_call_target="tpu_custom_call" | custom-call | tf_op jit(solution)/shard_map/nmf/pallas_call | solution.py:418
  488.8 0.0 copy-start
  488.8 4.6 copy.7
  493.4 0.0 copy-done
  493.4 2.0 copy.8
Async XLA Ops:
  488.8 4.7 copy-start

commit v6 on v5

--- a/solution.py
+++ b/solution.py
@@ -12,6 +12,7 @@
 ND = 8
 NV = 8
 GROUP = 4
+S_OTHER = 4
 LAG1, LAG2, LAG3, LAG5 = 2, 4, 5, 6
 LANES = 128
 MESH = pl.DeviceIdType.MESH
@@ -23,6 +24,7 @@
     rows, cols, c_hbm, w_hbm, h_hbm, w_out, h_out,
     c_v, w_bf, w_t, h_bf, h_t, w_f, h_f, a_w, a_h, r_a, r_x, r_y,
     sw_acc, sw_slots, sw_col, sh_acc, sh_part, sh_slots, sh_row,
+    c_two, w_two, a_s, h_s, c_send, c_recv, u_send, u_recv, b_send, b_recv, s_sems, os_sem,
     w_sem, h_sem, c_sem,
     a_send, a_recv, x_send, x_recv, g_send, g_recv, p_send, p_recv, q_send, q_recv,
     y_send, y_recv, z_send, z_recv, sw_send, sw_recv, sh_send, sh_recv,
@@ -32,6 +34,7 @@
     topics = w_bf.shape[1]
     dt, vt, kh = docs // ND, words // NV, topics // 2
     half, quarter = dt // 2, dt // 4
+    nr, vh = NV - 1, vt // 2
     n_dev = rows * cols
     y, i = lax.axis_index("row"), lax.axis_index("col")
     x, core = i // 2, i % 2
@@ -84,6 +87,31 @@
     def copy_z(v):
         return remote(h_bf.at[v, own_k], h_bf.at[v, own_k], z_send.at[v], z_recv.at[v], above)
 
+    def shared(side):
+        return rows_at(side * vh, vh)
+
+    def whole(side):
+        return rows_at(nr * vt + side * vh, vh)
+
+    def copy_c():
+        return remote(c_hbm.at[:, whole(1 - y)], c_two, c_send.at[0], c_recv.at[0], above)
+
+    def copy_u(d):
+        return remote(w_bf.at[mine(d)], w_two.at[d, core * 2 + x], u_send.at[d], u_recv.at[d], above)
+
+    def copy_b(step):
+        strip = w_two.at[:, core * 2 + x]
+        return remote(strip, strip, b_send.at[step - 1], b_recv.at[step - 1], {"col": (i + step) % cols})
+
+    def copy_zs():
+        return remote(h_bf.at[nr, :, shared(y)], h_bf.at[nr, :, shared(y)], s_sems.at[0], s_sems.at[1], above)
+
+    def copy_hs():
+        return remote(h_s, h_out.at[:, whole(y)], s_sems.at[2], s_sems.at[3], above)
+
+    def out_s():
+        return pltpu.make_async_copy(h_s, h_out.at[:, whole(y)], os_sem.at[0])
+
     def copy_sw(step):
         return remote(sw_acc, sw_slots.at[me], sw_send.at[step - 1], sw_recv.at[step - 1], peer(step))
 
@@ -132,6 +160,19 @@
         held = a_h[v]
         a_h[v] = select(d == 0, held) + part
 
+    def s_tile(d, rows_bf, counts, first):
+        z = jnp.dot(rows_bf, h_bf[nr, :, shared(y)], preferred_element_type=F32)
+        q = (counts.astype(F32) / (z + EPS)).astype(BF16)
+        part = jnp.dot(rows_bf.T, q, preferred_element_type=F32)
+        a_s[...] = (jnp.where(d == 0, 0.0, a_s[...]) if first else a_s[...]) + part
+
+    def s_own(d):
+        at = rows_at(d * dt, dt)
+        s_tile(d, w_bf[at, :], c_v[at, whole(y)], True)
+
+    def s_other(d):
+        s_tile(d, w_two[d].reshape(dt, topics), c_two[rows_at(d * dt, dt), :], False)
+
     def fold_lanes(block):
         total = block[:, :LANES]
         for g in range(1, block.shape[1] // LANES):
@@ -139,7 +180,9 @@
         return total
 
     def send_sh():
-        sh_part[...] = jnp.sum(sh_acc[...].T.reshape(LANES // 8, 8, kh), axis=0)
+        for r in range(rows):
+            at = slice(r * kh, (r + 1) * kh)
+            sh_part[:, at] = jnp.sum(sh_acc[at, :].T.reshape(LANES // 8, 8, kh), axis=0)
         sh_slots[me] = sh_part[...]
         for step in range(1, n_dev):
             copy_sh(step).start()
@@ -147,11 +190,10 @@
     def take_sh():
         for step in range(1, n_dev):
             copy_sh(step).wait()
-        for r in range(rows):
-            total = sh_slots[r * cols]
-            for n in range(1, cols):
-                total = total + sh_slots[r * cols + n]
-            sh_row[:, r * kh:(r + 1) * kh] = jnp.broadcast_to(jnp.sum(total, axis=0, keepdims=True), (8, kh))
+        total = sh_slots[0]
+        for n in range(1, n_dev):
+            total = total + sh_slots[n]
+        sh_row[...] = jnp.broadcast_to(jnp.sum(total, axis=0, keepdims=True), (8, topics))
 
     def send_sw():
         sw_slots[me] = sw_acc[...]
@@ -165,8 +207,9 @@
         for n in range(1, n_dev):
             total = total + sw_slots[n]
         total = jnp.sum(total, axis=0, keepdims=True)
-        own = jnp.where(y == 0, total[:, :kh], total[:, kh:])
-        sw_col[...] = jnp.broadcast_to(own, (LANES, kh)).T
+        for r in range(rows):
+            at = slice(r * kh, (r + 1) * kh)
+            sw_col[at, :] = jnp.broadcast_to(total[:, at], (LANES, kh)).T
 
     def load_h(v):
         return pltpu.make_async_copy(h_hbm.at[:, words_at(v)], a_h.at[v], h_sem.at[v])
@@ -185,10 +228,19 @@
     def start_h(v):
         load_h(v).wait()
         h_bf[v] = a_h[v].astype(BF16)
-        own = a_h[v, own_k]
-        h_f[v] = own
-        sh_acc[...] += fold_lanes(own)
         h_t[words_at(v), :] = h_bf[v].T
+
+        @pl.when(v < nr)
+        def _():
+            own = a_h[v, own_k]
+            h_f[v] = own
+            sh_acc[own_k, :] += fold_lanes(own)
+
+        @pl.when(v == nr)
+        def _():
+            own = a_h[nr, :, shared(y)]
+            h_s[...] = own
+            sh_acc[...] += fold_lanes(own)
 
         @pl.when(v + 1 < ND)
         def _():
@@ -198,6 +250,7 @@
     each(NV, start_h)
     pl.semaphore_wait(barrier, n_dev - 1)
     send_sh()
+    copy_c().start()
 
     def start_w(d):
         load_w(d).wait()
@@ -217,7 +270,7 @@
 
             @pl.when(sweep > 0)
             def _():
-                w_tile(d, NV - 1)
+                w_tile(d, nr - 1)
             copy_a(d).start()
 
         def s1(d):
@@ -238,6 +291,10 @@
             w_bf[mine(d), :] = fresh.astype(BF16)
             copy_g(d).start()
             copy_p(d).start()
+
+            @pl.when(sweep > 0)
+            def _():
+                copy_u(d).start()
             sw_acc[...] += jnp.sum(fresh.reshape(quarter // 8, 8, topics), axis=0)
 
             @pl.when(d == ND - 1)
@@ -255,20 +312,17 @@
 
             @pl.when(d < ND - 1)
             def _():
-                for v in range(NV):
+                for v in range(nr):
                     h_tile(d, v)
 
             @pl.when(d == ND - 1)
             def _():
-                def group(n):
-                    h_tile(d, 2 * n)
-                    h_tile(d, 2 * n + 1)
-
-                    @pl.when(n == 0)
-                    def _():
-                        copy_y(0).start()
-                        copy_y(1).start()
-                each(NV // 2, group)
+                h_tile(d, 0)
+                h_tile(d, 1)
+                copy_y(0).start()
+                copy_y(1).start()
+                for v in range(2, nr):
+                    h_tile(d, v)
 
         def stage(it, lag, body):
             @pl.when(jnp.logical_and(it >= lag, it < lag + ND))
@@ -306,16 +360,16 @@
             copy_y(v).wait_recv()
             for g in range(vt // LANES):
                 at = slice(g * LANES, (g + 1) * LANES)
-                fresh = h_f[v, :, at] * (a_h[v, own_k, at] + r_y[v, :, at]) / sw_col[...]
+                fresh = h_f[v, :, at] * (a_h[v, own_k, at] + r_y[v, :, at]) / sw_col[own_k, :]
                 h_f[v, :, at] = fresh
                 h_bf[v, own_k, at] = fresh.astype(BF16)
-                sh_acc[...] += fresh
+                sh_acc[own_k, :] += fresh
 
             @pl.when(jnp.logical_not(last))
             def _():
                 copy_z(v).start()
 
-                @pl.when(v == NV - 1)
+                @pl.when(v == nr - 1)
                 def _():
                     send_sh()
 
@@ -324,23 +378,43 @@
                 out_h(v).start()
                 copy_ho(v).start()
 
-            @pl.when(v + 2 < NV)
+            @pl.when(v + 2 < nr)
             def _():
                 copy_y(v + 2).start()
+
+        def w_words(v):
+            def group(n):
+                for k in range(GROUP):
+                    w_tile(n * GROUP + k, v)
+            each(ND // GROUP, group)
 
         def t3(v):
             copy_z(v).wait_recv()
             h_t[words_at(v), :] = h_bf[v].T
 
-            @pl.when(v < NV - 1)
-            def _():
-                def group(n):
-                    for k in range(GROUP):
-                        w_tile(n * GROUP + k, v)
-                each(ND // GROUP, group)
+            @pl.when(v < nr - 1)
+            def _():
+                w_words(v)
+
+        def update_s():
+            for g in range(vh // LANES):
+                at = slice(g * LANES, (g + 1) * LANES)
+                fresh = h_s[:, at] * a_s[:, at] / sw_col[...]
+                h_s[:, at] = fresh
+                sh_acc[...] += fresh
+            h_bf[nr, :, shared(y)] = h_s[...].astype(BF16)
+
+            @pl.when(jnp.logical_not(last))
+            def _():
+                copy_zs().start()
+
+            @pl.when(last)
+            def _():
+                out_s().start()
+                copy_hs().start()
 
         def h_step(it):
-            @pl.when(it < NV)
+            @pl.when(it < nr)
             def _():
                 t1(it)
 
@@ -348,7 +422,37 @@
             def _():
                 t3(it - 1)
 
-        each(NV + 1, h_step)
+            @pl.when(it == 1)
+            def _():
+                each(ND, lambda d: copy_u(d).wait_recv())
+                for step in range(1, cols):
+                    copy_b(step).start()
+                each(ND, s_own)
+
+            @pl.when(it == S_OTHER)
+            def _():
+                @pl.when(sweep == 0)
+                def _():
+                    copy_c().wait()
+                for step in range(1, cols):
+                    copy_b(step).wait()
+                each(ND, s_other)
+
+            @pl.when(it == S_OTHER + 1)
+            def _():
+                update_s()
+
+            @pl.when(jnp.logical_and(it == nr - 1, jnp.logical_not(last)))
+            def _():
+                copy_zs().wait_recv()
+                h_t[words_at(nr), :] = h_bf[nr].T
+                w_words(nr)
+
+        @pl.when(sweep == 0)
+        def _():
+            each(ND, lambda d: copy_u(d).start())
+
+        each(nr + 1, h_step)
 
         def h_sent(v):
             copy_y(v).wait_send()
@@ -357,7 +461,12 @@
             def _():
                 copy_z(v).wait_send()
 
-        each(NV, h_sent)
+        each(nr, h_sent)
+        each(ND, lambda d: copy_u(d).wait_send())
+
+        @pl.when(jnp.logical_not(last))
+        def _():
+            copy_zs().wait_send()
         return carry
 
     lax.fori_loop(0, SWEEPS, sweep_body, 0)
@@ -372,7 +481,9 @@
         copy_ho(v).wait()
 
     each(ND, finish_w)
-    each(NV, finish_h)
+    each(nr, finish_h)
+    out_s().wait()
+    copy_hs().wait()
 
 
 def solution(mesh):
@@ -384,36 +495,35 @@
         topics = w_loc.shape[1]
         vmem = pltpu.VMEM
         dma = pltpu.SemaphoreType.DMA
+        chunk = words // NV
         scratch = [
             vmem((docs, words), BF16),
             vmem((docs, topics), BF16),
             vmem((topics, docs // ND), BF16),
-            vmem((NV, topics, words // NV), BF16),
+            vmem((NV, topics, chunk), BF16),
             vmem((words, topics), BF16),
             vmem((docs // 4, topics), F32),
-            vmem((NV, topics // 2, words // NV), F32),
+            vmem((NV - 1, topics // 2, chunk), F32),
             vmem((docs, topics), F32),
-            vmem((NV, topics, words // NV), F32),
+            vmem((NV, topics, chunk), F32),
             vmem((docs // 2, topics), F32),
             vmem((docs // 4, topics), F32),
-            vmem((NV, topics // 2, words // NV), F32),
+            vmem((NV - 1, topics // 2, chunk), F32),
             vmem((8, topics), F32),
             vmem((n_dev, 8, topics), F32),
-            vmem((topics // 2, LANES), F32),
-            vmem((topics // 2, LANES), F32),
-            vmem((8, topics // 2), F32),
-            vmem((n_dev, 8, topics // 2), F32),
+            vmem((topics, LANES), F32),
+            vmem((topics, LANES), F32),
             vmem((8, topics), F32),
-            dma((ND,)),
-            dma((NV,)),
-            dma((ND,)),
+            vmem((n_dev, 8, topics), F32),
+            vmem((8, topics), F32),
+            vmem((docs, chunk // 2), BF16),
+            vmem((ND, 4, docs // ND // 4, topics), BF16),
+            vmem((topics, chunk // 2), F32),
+            vmem((topics, chunk // 2), F32),
         ]
-        scratch += [dma((ND,))] * 10
-        scratch += [dma((NV,))] * 4
-        scratch += [dma((n_dev - 1,))] * 4
-        scratch += [dma((ND * (cols - 1),))] * 2
-        scratch += [dma((NV,))] * 2
-        scratch += [dma((ND,)), dma((NV,))]
+        sizes = [1, 1, ND, ND, cols - 1, cols - 1, 4, 1, ND, NV, ND]
+        sizes += [ND] * 10 + [NV] * 4 + [n_dev - 1] * 4 + [ND * (cols - 1)] * 2 + [NV] * 2 + [ND, NV]
+        scratch += [dma((size,)) for size in sizes]
         any_space = pl.BlockSpec(memory_space=pl.ANY)
         return pl.pallas_call(
             functools.partial(kernel, rows, cols),

time: 496 us -> 489 us (0.986)
  Pallas kernels: 488 us -> 482 us
    pallas_call x1, Pallas kernels: 488 us -> 482 us  [local(): pl.pallas_call(functools.partial(kernel, rows, cols), out_shape=(jax.Shap...]
where the time goes in v6:
time: 489 us
  Pallas kernels  482 us (99%)
  local copies, waits for them, and re-layouts  6.66 us (1%)
    pallas_call x1, Pallas kernels, local(): pl.pallas_call(functools.partial(kernel, rows, cols), out_shape=(jax.Shap...  482 us

profile of v6, /device:TPU:0, one launch (start us, length us, event | category | flops | bytes accessed | tf_op | source)
XLA Modules:
  0.0 489.0 jit_solution(11834751468276757907)
XLA Ops:
  0.6 481.7 %nmf.1 = (f32[4096,256]{1,0:T(8,128)}, f32[256,4096]{1,0:T(8,128)}) custom-call(bf16[4096,4096]{1,0:T(8,128)(2,1)} %c_hbm.1, f32[4096,256]{1,0:T(8,128)} %w_hbm.1, f32[256,4096]{1,0:T(8,128)} %h_hbm.1), custom_call_target="tpu_custom_call" | custom-call | tf_op jit(solution)/shard_map/nmf/pallas_call | solution.py:528
  482.3 0.0 copy-start
  482.3 4.6 copy.7
  487.0 0.0 copy-done
  487.0 2.0 copy.8
Async XLA Ops:
  482.3 4.7 copy-start

commit v7 on v6

--- a/solution.py
+++ b/solution.py
@@ -12,7 +12,7 @@
 ND = 8
 NV = 8
 GROUP = 4
-S_OTHER = 4
+S_OTHER = 3
 LAG1, LAG2, LAG3, LAG5 = 2, 4, 5, 6
 LANES = 128
 MESH = pl.DeviceIdType.MESH
@@ -344,13 +344,10 @@
 
         each(ND, w_sent)
 
-        @pl.when(last)
-        def _():
-            def give(d):
-                out_w(d).start()
-                for step in range(1, cols):
-                    copy_wo(d, step).start()
-            each(ND, give)
+        def give(d):
+            out_w(d).start()
+            for step in range(1, cols):
+                copy_wo(d, step).start()
 
         def t1(v):
             @pl.when(v == 0)
@@ -418,16 +415,15 @@
             def _():
                 t1(it)
 
-            @pl.when(jnp.logical_and(it >= 1, jnp.logical_not(last)))
-            def _():
-                t3(it - 1)
-
-            @pl.when(it == 1)
+            @pl.when(it == jnp.where(sweep == 0, 1, 0))
             def _():
                 each(ND, lambda d: copy_u(d).wait_recv())
                 for step in range(1, cols):
                     copy_b(step).start()
-                each(ND, s_own)
+
+                @pl.when(last)
+                def _():
+                    each(ND, give)
 
             @pl.when(it == S_OTHER)
             def _():
@@ -436,10 +432,11 @@
                     copy_c().wait()
                 for step in range(1, cols):
                     copy_b(step).wait()
-                each(ND, s_other)
+                each(ND // 2, s_other)
 
             @pl.when(it == S_OTHER + 1)
             def _():
+                each(ND // 2, lambda d: s_other(d + ND // 2))
                 update_s()
 
             @pl.when(jnp.logical_and(it == nr - 1, jnp.logical_not(last)))
@@ -448,10 +445,15 @@
                 h_t[words_at(nr), :] = h_bf[nr].T
                 w_words(nr)
 
+            @pl.when(jnp.logical_and(it >= 1, jnp.logical_not(last)))
+            def _():
+                t3(it - 1)
+
         @pl.when(sweep == 0)
         def _():
             each(ND, lambda d: copy_u(d).start())
 
+        each(ND, s_own)
         each(nr + 1, h_step)
 
         def h_sent(v):

time: 489 us -> 483 us (0.988)
  Pallas kernels: 482 us -> 476 us
    pallas_call x1, Pallas kernels: 482 us -> 476 us  [local(): pl.pallas_call(functools.partial(kernel, rows, cols), out_shape=(jax.Shap...]
where the time goes in v7:
time: 483 us
  Pallas kernels  476 us (99%)
  local copies, waits for them, and re-layouts  6.66 us (1%)
    pallas_call x1, Pallas kernels, local(): pl.pallas_call(functools.partial(kernel, rows, cols), out_shape=(jax.Shap...  476 us

profile of v7, /device:TPU:0, one launch (start us, length us, event | category | flops | bytes accessed | tf_op | source)
XLA Modules:
  0.0 482.8 jit_solution(17919625281455872608)
XLA Ops:
  0.6 475.5 %nmf.1 = (f32[4096,256]{1,0:T(8,128)}, f32[256,4096]{1,0:T(8,128)}) custom-call(bf16[4096,4096]{1,0:T(8,128)(2,1)} %c_hbm.1, f32[4096,256]{1,0:T(8,128)} %w_hbm.1, f32[256,4096]{1,0:T(8,128)} %h_hbm.1), custom_call_target="tpu_custom_call" | custom-call | tf_op jit(solution)/shard_map/nmf/pallas_call | solution.py:530
  476.2 0.0 copy-start
  476.2 4.6 copy.7
  480.8 0.0 copy-done
  480.8 2.0 copy.8
Async XLA Ops:
  476.2 4.7 copy-start

commit v8 on v7

--- a/solution.py
+++ b/solution.py
@@ -25,6 +25,7 @@
     c_v, w_bf, w_t, h_bf, h_t, w_f, h_f, a_w, a_h, r_a, r_x, r_y,
     sw_acc, sw_slots, sw_col, sh_acc, sh_part, sh_slots, sh_row,
     c_two, w_two, a_s, h_s, c_send, c_recv, u_send, u_recv, b_send, b_recv, s_sems, os_sem,
+    a_o, r_o, o_sems,
     w_sem, h_sem, c_sem,
     a_send, a_recv, x_send, x_recv, g_send, g_recv, p_send, p_recv, q_send, q_recv,
     y_send, y_recv, z_send, z_recv, sw_send, sw_recv, sh_send, sh_recv,
@@ -96,6 +97,9 @@
     def copy_c():
         return remote(c_hbm.at[:, whole(1 - y)], c_two, c_send.at[0], c_recv.at[0], above)
 
+    def copy_o():
+        return remote(a_o, r_o, o_sems.at[0], o_sems.at[1], above)
+
     def copy_u(d):
         return remote(w_bf.at[mine(d)], w_two.at[d, core * 2 + x], u_send.at[d], u_recv.at[d], above)
 
@@ -160,18 +164,22 @@
         held = a_h[v]
         a_h[v] = select(d == 0, held) + part
 
-    def s_tile(d, rows_bf, counts, first):
-        z = jnp.dot(rows_bf, h_bf[nr, :, shared(y)], preferred_element_type=F32)
+    def s_tile(total, rows_bf, counts, h_half, first):
+        z = jnp.dot(rows_bf, h_half, preferred_element_type=F32)
         q = (counts.astype(F32) / (z + EPS)).astype(BF16)
         part = jnp.dot(rows_bf.T, q, preferred_element_type=F32)
-        a_s[...] = (jnp.where(d == 0, 0.0, a_s[...]) if first else a_s[...]) + part
+        total[...] = jnp.where(first, 0.0, total[...]) + part
 
     def s_own(d):
         at = rows_at(d * dt, dt)
-        s_tile(d, w_bf[at, :], c_v[at, whole(y)], True)
+        s_tile(a_s, w_bf[at, :], c_v[at, whole(y)], h_bf[nr, :, shared(y)], d == 0)
+
+    def s_cross(d):
+        at = rows_at(d * dt, dt)
+        s_tile(a_o, w_bf[at, :], c_v[at, whole(1 - y)], h_bf[nr, :, shared(1 - y)], d == 0)
 
     def s_other(d):
-        s_tile(d, w_two[d].reshape(dt, topics), c_two[rows_at(d * dt, dt), :], False)
+        s_tile(a_s, w_two[d].reshape(dt, topics), c_two[rows_at(d * dt, dt), :], h_bf[nr, :, shared(y)], False)
 
     def fold_lanes(block):
         total = block[:, :LANES]
@@ -415,7 +423,7 @@
             def _():
                 t1(it)
 
-            @pl.when(it == jnp.where(sweep == 0, 1, 0))
+            @pl.when(jnp.logical_and(it == 0, sweep > 0))
             def _():
                 each(ND, lambda d: copy_u(d).wait_recv())
                 for step in range(1, cols):
@@ -425,9 +433,14 @@
                 def _():
                     each(ND, give)
 
-            @pl.when(it == S_OTHER)
-            def _():
-                @pl.when(sweep == 0)
+            @pl.when(jnp.logical_and(it == S_OTHER, sweep == 0))
+            def _():
+                copy_o().wait()
+                a_s[...] += r_o[...]
+
+            @pl.when(jnp.logical_and(it == S_OTHER, sweep > 0))
+            def _():
+                @pl.when(sweep == 1)
                 def _():
                     copy_c().wait()
                 for step in range(1, cols):
@@ -436,7 +449,9 @@
 
             @pl.when(it == S_OTHER + 1)
             def _():
-                each(ND // 2, lambda d: s_other(d + ND // 2))
+                @pl.when(sweep > 0)
+                def _():
+                    each(ND // 2, lambda d: s_other(d + ND // 2))
                 update_s()
 
             @pl.when(jnp.logical_and(it == nr - 1, jnp.logical_not(last)))
@@ -451,7 +466,8 @@
 
         @pl.when(sweep == 0)
         def _():
-            each(ND, lambda d: copy_u(d).start())
+            each(ND, s_cross)
+            copy_o().start()
 
         each(ND, s_own)
         each(nr + 1, h_step)
@@ -464,7 +480,9 @@
                 copy_z(v).wait_send()
 
         each(nr, h_sent)
-        each(ND, lambda d: copy_u(d).wait_send())
+        @pl.when(sweep > 0)
+        def _():
+            each(ND, lambda d: copy_u(d).wait_send())
 
         @pl.when(jnp.logical_not(last))
         def _():
@@ -526,6 +544,8 @@
         sizes = [1, 1, ND, ND, cols - 1, cols - 1, 4, 1, ND, NV, ND]
         sizes += [ND] * 10 + [NV] * 4 + [n_dev - 1] * 4 + [ND * (cols - 1)] * 2 + [NV] * 2 + [ND, NV]
         scratch += [dma((size,)) for size in sizes]
+        extra = [vmem((topics, chunk // 2), F32), vmem((topics, chunk // 2), F32), dma((2,))]
+        scratch[31:31] = extra
         any_space = pl.BlockSpec(memory_space=pl.ANY)
         return pl.pallas_call(
             functools.partial(kernel, rows, cols),

time: 483 us -> 477 us (0.988)
  Pallas kernels: 476 us -> 470 us
    pallas_call x1, Pallas kernels: 476 us -> 470 us  [local(): pl.pallas_call(functools.partial(kernel, rows, cols), out_shape=(jax.Shap...]
where the time goes in v8:
time: 477 us
  Pallas kernels  470 us (99%)
  local copies, waits for them, and re-layouts  6.66 us (1%)
    pallas_call x1, Pallas kernels, local(): pl.pallas_call(functools.partial(kernel, rows, cols), out_shape=(jax.Shap...  470 us

profile of v8, /device:TPU:0, one launch (start us, length us, event | category | flops | bytes accessed | tf_op | source)
XLA Modules:
  0.0 477.2 jit_solution(17310238611892748543)
XLA Ops:
  0.6 469.9 %nmf.1 = (f32[4096,256]{1,0:T(8,128)}, f32[256,4096]{1,0:T(8,128)}) custom-call(bf16[4096,4096]{1,0:T(8,128)(2,1)} %c_hbm.1, f32[4096,256]{1,0:T(8,128)} %w_hbm.1, f32[256,4096]{1,0:T(8,128)} %h_hbm.1), custom_call_target="tpu_custom_call" | custom-call | tf_op jit(solution)/shard_map/nmf/pallas_call | solution.py:550
  470.6 0.0 copy-start
  470.6 4.6 copy.7
  475.2 0.0 copy-done
  475.2 2.0 copy.8
Async XLA Ops:
  470.6 4.7 copy-start

commit v9 on v8

--- a/solution.py
+++ b/solution.py
@@ -12,6 +12,7 @@
 ND = 8
 NV = 8
 GROUP = 4
+NS = 2
 S_OTHER = 3
 LAG1, LAG2, LAG3, LAG5 = 2, 4, 5, 6
 LANES = 128
@@ -35,7 +36,7 @@
     topics = w_bf.shape[1]
     dt, vt, kh = docs // ND, words // NV, topics // 2
     half, quarter = dt // 2, dt // 4
-    nr, vh = NV - 1, vt // 2
+    nr, vh = NV - NS, vt // 2
     n_dev = rows * cols
     y, i = lax.axis_index("row"), lax.axis_index("col")
     x, core = i // 2, i % 2
@@ -91,14 +92,15 @@
     def shared(side):
         return rows_at(side * vh, vh)
 
-    def whole(side):
-        return rows_at(nr * vt + side * vh, vh)
-
-    def copy_c():
-        return remote(c_hbm.at[:, whole(1 - y)], c_two, c_send.at[0], c_recv.at[0], above)
-
-    def copy_o():
-        return remote(a_o, r_o, o_sems.at[0], o_sems.at[1], above)
+    def whole(k, side):
+        return rows_at((NV - 1 - k) * vt + side * vh, vh)
+
+    def copy_c(k, d):
+        at = rows_at(d * dt, dt)
+        return remote(c_hbm.at[at, whole(k, 1 - y)], c_two.at[k, at], c_send.at[k, d], c_recv.at[k, d], above)
+
+    def copy_o(k):
+        return remote(a_o.at[k], r_o.at[k], o_sems.at[k, 0], o_sems.at[k, 1], above)
 
     def copy_u(d):
         return remote(w_bf.at[mine(d)], w_two.at[d, core * 2 + x], u_send.at[d], u_recv.at[d], above)
@@ -107,14 +109,15 @@
         strip = w_two.at[:, core * 2 + x]
         return remote(strip, strip, b_send.at[step - 1], b_recv.at[step - 1], {"col": (i + step) % cols})
 
-    def copy_zs():
-        return remote(h_bf.at[nr, :, shared(y)], h_bf.at[nr, :, shared(y)], s_sems.at[0], s_sems.at[1], above)
-
-    def copy_hs():
-        return remote(h_s, h_out.at[:, whole(y)], s_sems.at[2], s_sems.at[3], above)
-
-    def out_s():
-        return pltpu.make_async_copy(h_s, h_out.at[:, whole(y)], os_sem.at[0])
+    def copy_zs(k):
+        part = h_bf.at[NV - 1 - k, :, shared(y)]
+        return remote(part, part, s_sems.at[k, 0], s_sems.at[k, 1], above)
+
+    def copy_hs(k):
+        return remote(h_s.at[k], h_out.at[:, whole(k, y)], s_sems.at[k, 2], s_sems.at[k, 3], above)
+
+    def out_s(k):
+        return pltpu.make_async_copy(h_s.at[k], h_out.at[:, whole(k, y)], os_sem.at[k])
 
     def copy_sw(step):
         return remote(sw_acc, sw_slots.at[me], sw_send.at[step - 1], sw_recv.at[step - 1], peer(step))
@@ -170,16 +173,17 @@
         part = jnp.dot(rows_bf.T, q, preferred_element_type=F32)
         total[...] = jnp.where(first, 0.0, total[...]) + part
 
-    def s_own(d):
+    def s_own(k, d):
         at = rows_at(d * dt, dt)
-        s_tile(a_s, w_bf[at, :], c_v[at, whole(y)], h_bf[nr, :, shared(y)], d == 0)
-
-    def s_cross(d):
+        s_tile(a_s.at[k], w_bf[at, :], c_v[at, whole(k, y)], h_bf[NV - 1 - k, :, shared(y)], d == 0)
+
+    def s_cross(k, d):
         at = rows_at(d * dt, dt)
-        s_tile(a_o, w_bf[at, :], c_v[at, whole(1 - y)], h_bf[nr, :, shared(1 - y)], d == 0)
-
-    def s_other(d):
-        s_tile(a_s, w_two[d].reshape(dt, topics), c_two[rows_at(d * dt, dt), :], h_bf[nr, :, shared(y)], False)
+        s_tile(a_o.at[k], w_bf[at, :], c_v[at, whole(k, 1 - y)], h_bf[NV - 1 - k, :, shared(1 - y)], d == 0)
+
+    def s_other(k, d):
+        counts = c_two[k, rows_at(d * dt, dt), :]
+        s_tile(a_s.at[k], w_two[d].reshape(dt, topics), counts, h_bf[NV - 1 - k, :, shared(y)], False)
 
     def fold_lanes(block):
         total = block[:, :LANES]
@@ -244,10 +248,10 @@
             h_f[v] = own
             sh_acc[own_k, :] += fold_lanes(own)
 
-        @pl.when(v == nr)
+        @pl.when(v >= nr)
         def _():
-            own = a_h[nr, :, shared(y)]
-            h_s[...] = own
+            own = a_h[v, :, shared(y)]
+            h_s[NV - 1 - v] = own
             sh_acc[...] += fold_lanes(own)
 
         @pl.when(v + 1 < ND)
@@ -258,7 +262,7 @@
     each(NV, start_h)
     pl.semaphore_wait(barrier, n_dev - 1)
     send_sh()
-    copy_c().start()
+    each(ND, lambda d: copy_c(0, d).start())
 
     def start_w(d):
         load_w(d).wait()
@@ -303,6 +307,11 @@
             @pl.when(sweep > 0)
             def _():
                 copy_u(d).start()
+
+            for k in range(1, NS):
+                @pl.when(jnp.logical_and(jnp.logical_or(sweep == k, sweep == k + 1), d < ND // 2))
+                def _(k=k):
+                    copy_c(k, (sweep - k) * (ND // 2) + d).start()
             sw_acc[...] += jnp.sum(fresh.reshape(quarter // 8, 8, topics), axis=0)
 
             @pl.when(d == ND - 1)
@@ -401,22 +410,35 @@
             def _():
                 w_words(v)
 
-        def update_s():
+        def update_s(k):
             for g in range(vh // LANES):
                 at = slice(g * LANES, (g + 1) * LANES)
-                fresh = h_s[:, at] * a_s[:, at] / sw_col[...]
-                h_s[:, at] = fresh
+                fresh = h_s[k, :, at] * a_s[k, :, at] / sw_col[...]
+                h_s[k, :, at] = fresh
                 sh_acc[...] += fresh
-            h_bf[nr, :, shared(y)] = h_s[...].astype(BF16)
+            h_bf[NV - 1 - k, :, shared(y)] = h_s[k].astype(BF16)
 
             @pl.when(jnp.logical_not(last))
             def _():
-                copy_zs().start()
+                copy_zs(k).start()
 
             @pl.when(last)
             def _():
-                out_s().start()
-                copy_hs().start()
+                out_s(k).start()
+                copy_hs(k).start()
+
+        def whole_sum(k):
+            @pl.when(sweep <= k)
+            def _():
+                copy_o(k).wait()
+                a_s[k] += r_o[k]
+
+            @pl.when(sweep > k)
+            def _():
+                @pl.when(sweep == k + 1)
+                def _():
+                    each(ND, lambda d: copy_c(k, d).wait())
+                each(ND, lambda d: s_other(k, d))
 
         def h_step(it):
             @pl.when(it < nr)
@@ -433,43 +455,40 @@
                 def _():
                     each(ND, give)
 
-            @pl.when(jnp.logical_and(it == S_OTHER, sweep == 0))
-            def _():
-                copy_o().wait()
-                a_s[...] += r_o[...]
-
             @pl.when(jnp.logical_and(it == S_OTHER, sweep > 0))
             def _():
-                @pl.when(sweep == 1)
-                def _():
-                    copy_c().wait()
                 for step in range(1, cols):
                     copy_b(step).wait()
-                each(ND // 2, s_other)
-
-            @pl.when(it == S_OTHER + 1)
-            def _():
-                @pl.when(sweep > 0)
-                def _():
-                    each(ND // 2, lambda d: s_other(d + ND // 2))
-                update_s()
+
+            for k in range(NS):
+                @pl.when(it == S_OTHER + k)
+                def _(k=k):
+                    whole_sum(k)
+
+            @pl.when(it == S_OTHER + NS - 1)
+            def _():
+                for k in range(NS):
+                    update_s(k)
+
+            @pl.when(jnp.logical_and(it >= 1, jnp.logical_not(last)))
+            def _():
+                t3(it - 1)
 
             @pl.when(jnp.logical_and(it == nr - 1, jnp.logical_not(last)))
             def _():
-                copy_zs().wait_recv()
-                h_t[words_at(nr), :] = h_bf[nr].T
-                w_words(nr)
-
-            @pl.when(jnp.logical_and(it >= 1, jnp.logical_not(last)))
-            def _():
-                t3(it - 1)
-
-        @pl.when(sweep == 0)
-        def _():
-            each(ND, s_cross)
-            copy_o().start()
-
-        each(ND, s_own)
+                for k in range(NS):
+                    copy_zs(k).wait_recv()
+                    h_t[words_at(NV - 1 - k), :] = h_bf[NV - 1 - k].T
+                    w_words(NV - 1 - k)
+
+        for k in range(NS):
+            @pl.when(sweep <= k)
+            def _(k=k):
+                each(ND, lambda d: s_cross(k, d))
+                copy_o(k).start()
+
+        for k in range(NS):
+            each(ND, lambda d: s_own(k, d))
         each(nr + 1, h_step)
 
         def h_sent(v):
@@ -486,7 +505,8 @@
 
         @pl.when(jnp.logical_not(last))
         def _():
-            copy_zs().wait_send()
+            for k in range(NS):
+                copy_zs(k).wait_send()
         return carry
 
     lax.fori_loop(0, SWEEPS, sweep_body, 0)
@@ -502,8 +522,9 @@
 
     each(ND, finish_w)
     each(nr, finish_h)
-    out_s().wait()
-    copy_hs().wait()
+    for k in range(NS):
+        out_s(k).wait()
+        copy_hs(k).wait()
 
 
 def solution(mesh):
@@ -523,12 +544,12 @@
             vmem((NV, topics, chunk), BF16),
             vmem((words, topics), BF16),
             vmem((docs // 4, topics), F32),
-            vmem((NV - 1, topics // 2, chunk), F32),
+            vmem((NV - NS, topics // 2, chunk), F32),
             vmem((docs, topics), F32),
             vmem((NV, topics, chunk), F32),
             vmem((docs // 2, topics), F32),
             vmem((docs // 4, topics), F32),
-            vmem((NV - 1, topics // 2, chunk), F32),
+            vmem((NV - NS, topics // 2, chunk), F32),
             vmem((8, topics), F32),
             vmem((n_dev, 8, topics), F32),
             vmem((topics, LANES), F32),
@@ -536,15 +557,15 @@
             vmem((8, topics), F32),
             vmem((n_dev, 8, topics), F32),
             vmem((8, topics), F32),
-            vmem((docs, chunk // 2), BF16),
+            vmem((NS, docs, chunk // 2), BF16),
             vmem((ND, 4, docs // ND // 4, topics), BF16),
-            vmem((topics, chunk // 2), F32),
-            vmem((topics, chunk // 2), F32),
+            vmem((NS, topics, chunk // 2), F32),
+            vmem((NS, topics, chunk // 2), F32),
         ]
-        sizes = [1, 1, ND, ND, cols - 1, cols - 1, 4, 1, ND, NV, ND]
+        sizes = [(NS, ND)] * 2 + [ND, ND, cols - 1, cols - 1, (NS, 4), NS, ND, NV, ND]
         sizes += [ND] * 10 + [NV] * 4 + [n_dev - 1] * 4 + [ND * (cols - 1)] * 2 + [NV] * 2 + [ND, NV]
-        scratch += [dma((size,)) for size in sizes]
-        extra = [vmem((topics, chunk // 2), F32), vmem((topics, chunk // 2), F32), dma((2,))]
+        scratch += [dma(size if isinstance(size, tuple) else (size,)) for size in sizes]
+        extra = [vmem((NS, topics, chunk // 2), F32), vmem((NS, topics, chunk // 2), F32), dma((NS, 2))]
         scratch[31:31] = extra
         any_space = pl.BlockSpec(memory_space=pl.ANY)
         return pl.pallas_call(

time: 477 us -> 463 us (0.971)
  Pallas kernels: 470 us -> 456 us
    pallas_call x1, Pallas kernels: 470 us -> 456 us  [local(): pl.pallas_call(functools.partial(kernel, rows, cols), out_shape=(jax.Shap...]
where the time goes in v9:
time: 463 us
  Pallas kernels  456 us (98%)
  local copies, waits for them, and re-layouts  6.66 us (1%)
    pallas_call x1, Pallas kernels, local(): pl.pallas_call(functools.partial(kernel, rows, cols), out_shape=(jax.Shap...  456 us

profile of v9, /device:TPU:0, one launch (start us, length us, event | category | flops | bytes accessed | tf_op | source)
XLA Modules:
  0.0 463.2 jit_solution(15211891210685800997)
XLA Ops:
  0.6 455.9 %nmf.1 = (f32[4096,256]{1,0:T(8,128)}, f32[256,4096]{1,0:T(8,128)}) custom-call(bf16[4096,4096]{1,0:T(8,128)(2,1)} %c_hbm.1, f32[4096,256]{1,0:T(8,128)} %w_hbm.1, f32[256,4096]{1,0:T(8,128)} %h_hbm.1), custom_call_target="tpu_custom_call" | custom-call | tf_op jit(solution)/shard_map/nmf/pallas_call | solution.py:571
  456.5 0.0 copy-start
  456.5 4.6 %copy.7 = f32[4096,256]{1,0:T(8,128)} copy(f32[4096,256]{1,0:T(8,128)} %get-tuple-element.4) | data formatting | bytes 8388608
  461.1 0.0 copy-done
  461.1 2.0 copy.8
Async XLA Ops:
  456.5 4.7 %copy-start = (f32[256,4096]{1,0:T(8,128)S(1)}, f32[256,4096]{1,0:T(8,128)}, u32[]{:S(2)}) copy-start(f32[256,4096]{1,0:T(8,128)} %get-tuple-element.5) | copy-start | bytes 12582916

commit v10 on v9

--- a/solution.py
+++ b/solution.py
@@ -12,7 +12,8 @@
 ND = 8
 NV = 8
 GROUP = 4
-NS = 2
+NS = 3
+PIECES = {1: (0, 6), 2: (6, 5), 3: (11, 5)}
 S_OTHER = 3
 LAG1, LAG2, LAG3, LAG5 = 2, 4, 5, 6
 LANES = 128
@@ -27,7 +28,7 @@
     sw_acc, sw_slots, sw_col, sh_acc, sh_part, sh_slots, sh_row,
     c_two, w_two, a_s, h_s, c_send, c_recv, u_send, u_recv, b_send, b_recv, s_sems, os_sem,
     a_o, r_o, o_sems,
-    w_sem, h_sem, c_sem,
+    w_sem, h_sem, hs_sem, c_sem,
     a_send, a_recv, x_send, x_recv, g_send, g_recv, p_send, p_recv, q_send, q_recv,
     y_send, y_recv, z_send, z_recv, sw_send, sw_recv, sh_send, sh_recv,
     wo_send, wo_recv, ho_send, ho_recv, ow_sem, oh_sem,
@@ -226,13 +227,20 @@
     def load_h(v):
         return pltpu.make_async_copy(h_hbm.at[:, words_at(v)], a_h.at[v], h_sem.at[v])
 
+    def load_s(k, side):
+        half_h = (a_o, r_o)[side].at[k]
+        return pltpu.make_async_copy(h_hbm.at[:, whole(k, side)], half_h, hs_sem.at[k, side])
+
     def load_w(d):
         return pltpu.make_async_copy(w_hbm.at[rows_at(d * dt, dt)], a_w.at[rows_at(d * dt, dt)], w_sem.at[d])
 
     barrier = pltpu.get_barrier_semaphore()
     for step in range(1, n_dev):
         pl.semaphore_signal(barrier, inc=1, device_id=peer(step), device_id_type=MESH)
-    each(NV, lambda v: load_h(v).start())
+    each(nr, lambda v: load_h(v).start())
+    for k in range(NS):
+        for side in range(rows):
+            load_s(k, side).start()
     load_w(0).start()
     load_c(0).start()
     sh_acc[...] = jnp.zeros_like(sh_acc)
@@ -241,25 +249,25 @@
         load_h(v).wait()
         h_bf[v] = a_h[v].astype(BF16)
         h_t[words_at(v), :] = h_bf[v].T
-
-        @pl.when(v < nr)
-        def _():
-            own = a_h[v, own_k]
-            h_f[v] = own
-            sh_acc[own_k, :] += fold_lanes(own)
-
-        @pl.when(v >= nr)
-        def _():
-            own = a_h[v, :, shared(y)]
-            h_s[NV - 1 - v] = own
-            sh_acc[...] += fold_lanes(own)
-
-        @pl.when(v + 1 < ND)
-        def _():
-            load_w(v + 1).start()
-            load_c(v + 1).start()
-
-    each(NV, start_h)
+        own = a_h[v, own_k]
+        h_f[v] = own
+        sh_acc[own_k, :] += fold_lanes(own)
+        load_w(v + 1).start()
+        load_c(v + 1).start()
+
+    each(nr, start_h)
+    for d in range(nr + 1, ND):
+        load_w(d).start()
+        load_c(d).start()
+    for k in range(NS):
+        for side in range(rows):
+            load_s(k, side).wait()
+            h_bf[NV - 1 - k, :, side * vh:(side + 1) * vh] = (a_o, r_o)[side][k].astype(BF16)
+        h_t[words_at(NV - 1 - k), :] = h_bf[NV - 1 - k].T
+        own = jnp.where(y == 0, a_o[k], r_o[k])
+        h_s[k] = own
+        sh_acc[...] += fold_lanes(own)
+
     pl.semaphore_wait(barrier, n_dev - 1)
     send_sh()
     each(ND, lambda d: copy_c(0, d).start())
@@ -284,6 +292,12 @@
             def _():
                 w_tile(d, nr - 1)
             copy_a(d).start()
+
+            for when, (base, count) in PIECES.items():
+                @pl.when(jnp.logical_and(sweep == when, d < count))
+                def _(base=base):
+                    piece = base + d
+                    copy_c(1 + piece // ND, piece % ND).start()
 
         def s1(d):
             copy_a(d).wait_recv()
@@ -308,10 +322,6 @@
             def _():
                 copy_u(d).start()
 
-            for k in range(1, NS):
-                @pl.when(jnp.logical_and(jnp.logical_or(sweep == k, sweep == k + 1), d < ND // 2))
-                def _(k=k):
-                    copy_c(k, (sweep - k) * (ND // 2) + d).start()
             sw_acc[...] += jnp.sum(fresh.reshape(quarter // 8, 8, topics), axis=0)
 
             @pl.when(d == ND - 1)
@@ -383,10 +393,6 @@
             def _():
                 copy_z(v).start()
 
-                @pl.when(v == nr - 1)
-                def _():
-                    send_sh()
-
             @pl.when(last)
             def _():
                 out_h(v).start()
@@ -460,15 +466,25 @@
                 for step in range(1, cols):
                     copy_b(step).wait()
 
-            for k in range(NS):
-                @pl.when(it == S_OTHER + k)
-                def _(k=k):
+            @pl.when(it == 1)
+            def _():
+                for k in range(2, NS):
+                    each(ND, lambda d: s_own(k, d))
+
+            @pl.when(it == S_OTHER)
+            def _():
+                for k in range(NS - 1):
                     whole_sum(k)
 
-            @pl.when(it == S_OTHER + NS - 1)
-            def _():
+            @pl.when(it == nr - 1)
+            def _():
+                whole_sum(NS - 1)
                 for k in range(NS):
                     update_s(k)
+
+                @pl.when(jnp.logical_not(last))
+                def _():
+                    send_sh()
 
             @pl.when(jnp.logical_and(it >= 1, jnp.logical_not(last)))
             def _():
@@ -487,7 +503,7 @@
                 each(ND, lambda d: s_cross(k, d))
                 copy_o(k).start()
 
-        for k in range(NS):
+        for k in range(2):
             each(ND, lambda d: s_own(k, d))
         each(nr + 1, h_step)
 
@@ -546,7 +562,7 @@
             vmem((docs // 4, topics), F32),
             vmem((NV - NS, topics // 2, chunk), F32),
             vmem((docs, topics), F32),
-            vmem((NV, topics, chunk), F32),
+            vmem((NV - NS, topics, chunk), F32),
             vmem((docs // 2, topics), F32),
             vmem((docs // 4, topics), F32),
             vmem((NV - NS, topics // 2, chunk), F32),
@@ -562,7 +578,7 @@
             vmem((NS, topics, chunk // 2), F32),
             vmem((NS, topics, chunk // 2), F32),
         ]
-        sizes = [(NS, ND)] * 2 + [ND, ND, cols - 1, cols - 1, (NS, 4), NS, ND, NV, ND]
+        sizes = [(NS, ND)] * 2 + [ND, ND, cols - 1, cols - 1, (NS, 4), NS, ND, NV, (NS, rows), ND]
         sizes += [ND] * 10 + [NV] * 4 + [n_dev - 1] * 4 + [ND * (cols - 1)] * 2 + [NV] * 2 + [ND, NV]
         scratch += [dma(size if isinstance(size, tuple) else (size,)) for size in sizes]
         extra = [vmem((NS, topics, chunk // 2), F32), vmem((NS, topics, chunk // 2), F32), dma((NS, 2))]

time: 463 us -> 474 us (1.024)
  Pallas kernels: 456 us -> 466 us
    pallas_call x1, Pallas kernels: 456 us -> 466 us  [local(): pl.pallas_call(functools.partial(kernel, rows, cols), out_shape=(jax.Shap...]
where the time goes in v10:
time: 474 us
  Pallas kernels  466 us (98%)
  local copies, waits for them, and re-layouts  6.66 us (1%)
    pallas_call x1, Pallas kernels, local(): pl.pallas_call(functools.partial(kernel, rows, cols), out_shape=(jax.Shap...  466 us

profile of v10, /device:TPU:0, one launch (start us, length us, event | category | flops | bytes accessed | tf_op | source)
XLA Modules:
  0.0 473.7 jit_solution(6011326560032093493)
XLA Ops:
  0.6 466.4 %nmf.1 = (f32[4096,256]{1,0:T(8,128)}, f32[256,4096]{1,0:T(8,128)}) custom-call(bf16[4096,4096]{1,0:T(8,128)(2,1)} %c_hbm.1, f32[4096,256]{1,0:T(8,128)} %w_hbm.1, f32[256,4096]{1,0:T(8,128)} %h_hbm.1), custom_call_target="tpu_custom_call" | custom-call | tf_op jit(solution)/shard_map/nmf/pallas_call | solution.py:587
  467.1 0.0 copy-start
  467.1 4.6 copy.7
  471.7 0.0 copy-done
  471.7 2.0 copy.8
Async XLA Ops:
  467.1 4.7 copy-start

commit v11 on v9

--- a/solution.py
+++ b/solution.py
@@ -14,7 +14,7 @@
 GROUP = 4
 NS = 2
 S_OTHER = 3
-LAG1, LAG2, LAG3, LAG5 = 2, 4, 5, 6
+LAG1, LAG2, LAG3, LAG5 = 2, 4, 5, 7
 LANES = 128
 MESH = pl.DeviceIdType.MESH
 F32 = jnp.float32
@@ -347,7 +347,7 @@
                 body(it - lag)
 
         def w_step(it):
-            for lag, body in ((LAG2, s2), (LAG1, s1), (0, s0), (LAG3, s3), (LAG5, s5)):
+            for lag, body in ((LAG5, s5), (LAG2, s2), (LAG1, s1), (0, s0), (LAG3, s3)):
                 stage(it, lag, body)
 
         each(ND + LAG5, w_step)

time: 463 us -> 463 us (level)
  no operation moved by 1% of the time
where the time goes in v11:
time: 463 us
  Pallas kernels  456 us (98%)
  local copies, waits for them, and re-layouts  6.66 us (1%)
    pallas_call x1, Pallas kernels, local(): pl.pallas_call(functools.partial(kernel, rows, cols), out_shape=(jax.Shap...  456 us

profile of v11, /device:TPU:0, one launch (start us, length us, event | category | flops | bytes accessed | tf_op | source)
XLA Modules:
  0.0 463.2 jit_solution(7384410220906830823)
XLA Ops:
  0.6 455.9 %nmf.1 = (f32[4096,256]{1,0:T(8,128)}, f32[256,4096]{1,0:T(8,128)}) custom-call(bf16[4096,4096]{1,0:T(8,128)(2,1)} %c_hbm.1, f32[4096,256]{1,0:T(8,128)} %w_hbm.1, f32[256,4096]{1,0:T(8,128)} %h_hbm.1), custom_call_target="tpu_custom_call" | custom-call | tf_op jit(solution)/shard_map/nmf/pallas_call | solution.py:571
  456.5 0.0 copy-start
  456.5 4.6 %copy.7 = f32[4096,256]{1,0:T(8,128)} copy(f32[4096,256]{1,0:T(8,128)} %get-tuple-element.4) | data formatting | bytes 8388608
  461.2 0.0 copy-done
  461.2 2.0 copy.8
Async XLA Ops:
  456.5 4.7 %copy-start = (f32[256,4096]{1,0:T(8,128)S(1)}, f32[256,4096]{1,0:T(8,128)}, u32[]{:S(2)}) copy-start(f32[256,4096]{1,0:T(8,128)} %get-tuple-element.5) | copy-start | bytes 12582916
